TPU v7x, 256 devices: a whole 4x4x8 slice. The times are simulated.
256 devices in a mesh: patch: 64 (over x, z, core), rep: 4 (over y).
Axes of the slice: x: 4, y: 4, z: 8, core: 2. Of those that a mesh axis runs over, the one named last changes fastest.
Arguments:
- node_latents: bfloat16 [4, 24576, 512], P('rep', 'patch'), may hold values from -6 to 6
- edge_latents: bfloat16 [4, 81920, 512], P('rep', 'patch'), may hold values from -6 to 6
- targets: bfloat16 [4, 24576, 128], P('rep', 'patch'), may hold values from -6 to 6
- edge_weight_in: bfloat16 [1536, 512], replicated, may hold values from -0.15625 to 0.15625
- edge_weight_out: bfloat16 [512, 512], replicated, may hold values from -0.25 to 0.25
- node_weight_in: bfloat16 [1024, 512], replicated, may hold values from -0.1875 to 0.1875
- node_weight_out: bfloat16 [512, 512], replicated, may hold values from -0.25 to 0.25
- readout_weight: bfloat16 [512, 128], replicated, may hold values from -0.25 to 0.25
- send_rows: int32 [64, 96], P('patch'), may hold values from 0 to 383, as said below
- far_rows: int32 [64, 64], P('patch'), may hold values from 0 to 383, as said below
- edge_sender: int32 [81920], P('patch'), may hold values from 0 to 543
- edge_receiver: int32 [81920], P('patch'), may hold values from 0 to 383
- edge_count: int32 [64], P('patch'), may hold values from 80 to 1280, as said below
- land_mask: int32 [24576], P('patch'), may hold values 0 or 1
- lat_band: int32 [24576], P('patch'), may hold values from 0 to 720
Outputs:
- node_grad: bfloat16 [4, 24576, 512], P('rep', 'patch')
- edge_grad: bfloat16 [4, 81920, 512], P('rep', 'patch')
- grad_edge_in: float32 [1536, 512], P('patch')
- grad_edge_out: float32 [512, 512], P('patch')
- grad_node_in: float32 [1024, 512], P('patch')
- grad_node_out: float32 [512, 512], P('patch')
- grad_readout: float32 [512, 128], P('patch')
Inputs may be any that keep to these rules, and one draw needn't show every extreme that they name: `send_rows`: the 16 entries of a patch for one neighbour are distinct. `far_rows`: each patch sends exactly one node to every patch (itself included). `edge_count`: some patch has all 1280 edges live.
All inputs are finite; a program needn't handle non-finite values. No bound on the sum of `land_mask` on one device may be relied on, other than what follows from the above.
Results may differ from a plain program's by a relative error of at most 0.012.
Values may be sent and summed in bfloat16 or wider, within the bound.
A program may use at most 128 MiB of HBM per device.

v0:
```python
import functools

import jax
import jax.numpy as jnp
from jax import lax
from jax.experimental import pallas as pl
from jax.experimental.pallas import tpu as pltpu
from jax.sharding import Mesh
from jax.sharding import PartitionSpec as P

OCEAN = 32
BANDS = 721
PATCH = ("patch_0", "patch_1", "patch_2")
MESH = pl.DeviceIdType.MESH
D = 512
NODE = 384
EDGE = 1280
NEAR = 96
FAR = 64
EXT = 640
TABLE = EXT + NODE
TILE = 256
OFFSETS = (1, -1, 2, -2, 3, -3)
BF = jnp.bfloat16
F32 = jnp.float32


def dot(a, b):
    return jnp.dot(a, b, preferred_element_type=F32)


def dot_t(a, b):
    return lax.dot_general(a, b, (((1,), (1,)), ((), ())), preferred_element_type=F32)


def t_dot(a, b):
    return lax.dot_general(a, b, (((0,), (0,)), ((), ())), preferred_element_type=F32)


def patch_id(q):
    return {"patch_0": q // 16, "patch_1": (q // 2) % 8, "patch_2": q % 2}


def normalize(v):
    mean = jnp.mean(v, axis=-1, keepdims=True)
    centred = v - mean
    var = jnp.mean(centred * centred, axis=-1, keepdims=True)
    inverse = lax.rsqrt(var + 1e-05)
    return centred * inverse, inverse


def norm_back(g, y, inverse):
    first = jnp.mean(g, axis=-1, keepdims=True)
    second = jnp.mean(g * y, axis=-1, keepdims=True)
    return inverse * (g - first - y * second)


def columns(rows):
    wide = rows[0].shape[1]
    pad = [jnp.zeros((8 - len(rows), wide), F32)]
    return jnp.concatenate(rows + pad, axis=0).T


class Reducer:
    def __init__(self, refs, where):
        (self.start0, self.r0, self.w1, self.r1, self.w2, self.r2, self.w3,
         self.r3, self.w4, self.r4, self.send, self.recv) = refs
        self.x, self.y, self.z, self.c = where
        self.pending = []

    def copy(self, src, dst, k, device):
        one = pltpu.make_async_remote_copy(
            src_ref=src, dst_ref=dst, send_sem=self.send.at[k], recv_sem=self.recv.at[k],
            device_id=device, device_id_type=MESH,
        )
        one.start()
        self.pending.append(one)
        return one

    def pair(self):
        other = 1 - self.c
        self.c0 = [
            self.copy(self.start0.at[h, other], self.r0.at[h], h, {"patch_2": other})
            for h in range(2)
        ]

    def over_x(self, src, dst, k):
        out = []
        for d in range(1, 4):
            to = (self.x + d) % 4
            out.append(self.copy(src(to), dst(d - 1), k + d - 1, {"patch_0": to}))
        return out

    def over_y(self, src, dst, k):
        out = []
        for d in range(1, 4):
            to = (self.y + d) % 4
            out.append(self.copy(src(to), dst(d - 1), k + d - 1, {"rep": to}))
        return out

    def first(self):
        for h in range(2):
            self.c0[h].wait_recv()

            @pl.loop(0, 4)
            def _(i):
                mine = self.start0[h, self.c, i].astype(F32)
                self.w1[h, i] = (mine + self.r0[h, i].astype(F32)).astype(BF)

            if h == 0:
                self.c1a = self.over_x(lambda to: self.w1.at[0, to], lambda s: self.r1.at[0, s], 2)
            else:
                self.c1b = self.over_y(
                    lambda to: self.w1.at[1, :, to],
                    lambda s: self.r1.at[1, s],
                    5,
                )

    def second(self):
        for one in self.c1a:
            one.wait_recv()

        @pl.loop(0, 4)
        def _(y):
            acc = self.w1[0, self.x, y].astype(F32)
            for s in range(3):
                acc = acc + self.r1[0, s, y].astype(F32)
            self.w2[0, y] = acc.astype(BF)

        self.c2a = self.over_y(lambda to: self.w2.at[0, to], lambda s: self.r2.at[0, s], 8)
        for one in self.c1b:
            one.wait_recv()

        @pl.loop(0, 4)
        def _(i):
            acc = self.w1[1, i, self.y].astype(F32)
            for s in range(3):
                acc = acc + self.r1[1, s, i].astype(F32)
            self.w2[1, i] = acc.astype(BF)

        self.c2b = self.over_x(lambda to: self.w2.at[1, to], lambda s: self.r2.at[1, s], 11)

    def third(self):
        for h, (copies, mine) in enumerate(((self.c2a, self.y), (self.c2b, self.x))):
            for one in copies:
                one.wait_recv()
            acc = self.w2[h, mine].astype(F32)
            for s in range(3):
                acc = acc + self.r2[h, s].astype(F32)
            self.w3[:, h] = acc.astype(BF)
        self.c3 = []
        for d in range(1, 8):
            to = (self.z + d) % 8
            self.c3.append(self.copy(self.w3.at[to], self.r3.at[d - 1], 13 + d, {"patch_1": to}))

    def fourth(self):
        for one in self.c3:
            one.wait_recv()
        acc = self.w3[self.z].astype(F32)
        for s in range(7):
            acc = acc + self.r3[s].astype(F32)
        self.w4[...] = acc * (1.0 / (NODE * 64 * 4))
        self.c4 = []
        for d in range(1, 4):
            to = (self.y + d) % 4
            self.c4.append(self.copy(self.w4, self.r4.at[d - 1], 20 + d, {"rep": to}))

    def last(self):
        for one in self.c4:
            one.wait_recv()
        out = []
        own = self.w4[...]
        got = [self.r4[s] for s in range(3)]
        for y in range(4):
            tile = own
            for s in range(3):
                tile = jnp.where((self.y - s - 1 + 4) % 4 == y, got[s], tile)
            out.append(tile)
        return out

    def finish(self):
        for one in self.pending:
            one.wait_send()


def kernel(
    x_hbm, e_hbm, t_hbm, we_in_hbm, we_out_hbm, wn_in_hbm, wn_out_hbm, wr_hbm,
    send_ref, far_ref, sender_ref, receiver_ref, count_ref, land_ref, lat_ref,
    node_out, edge_out, gei_out, geo_out, gni_out, gno_out, gr_out,
    xe, e, tgt, we_in, we_out, wn_in, wn_out, wr, edge_res,
    near_src, near_got, far_src, far_got, back_near_src, back_near_got, back_far_src, back_far_got,
    onehot, onehot_t, own_near, own_far, proj, pre, hid, slope, msg, inv, ezg, epg, total, agg_grad, gsum, wgrad,
    *rest,
):
    dma_sem, out_sem, near_send, near_recv, far_send, far_recv = rest[:6]
    bnear_send, bnear_recv, bfar_send, bfar_recv = rest[6:10]
    group_a, group_b = rest[10:22], rest[22:34]
    ix, iz, ic, iy = (lax.axis_index(a) for a in (*PATCH, "rep"))
    me = ix * 16 + iz * 2 + ic

    loads = {}
    for k, (name, src, dst) in enumerate((
        ("x", x_hbm.at[0], xe.at[pl.ds(0, NODE)]),
        ("we_in", we_in_hbm, we_in),
        ("e", e_hbm.at[0], e),
        ("we_out", we_out_hbm, we_out),
        ("wn_in", wn_in_hbm, wn_in),
        ("wn_out", wn_out_hbm, wn_out),
        ("wr", wr_hbm, wr),
        ("t", t_hbm.at[0], tgt),
    )):
        loads[name] = pltpu.make_async_copy(src, dst, dma_sem.at[k])
        loads[name].start()

    barrier = pltpu.get_barrier_semaphore()

    @pl.loop(1, 64)
    def _(d):
        pl.semaphore_signal(barrier, inc=1, device_id=patch_id((me + d) % 64), device_id_type=MESH)

    for d in range(1, 4):
        pl.semaphore_signal(
            barrier, inc=1, device_id={"rep": (iy + d) % 4}, device_id_type=MESH
        )

    ids = lax.broadcasted_iota(jnp.int32, (NODE, NEAR), 0)
    own_near[...] = jnp.where(ids == send_ref[...], 1.0, 0.0).astype(BF)
    ids = lax.broadcasted_iota(jnp.int32, (NODE, FAR), 0)
    own_far[...] = jnp.where(ids == far_ref[...], 1.0, 0.0).astype(BF)
    loads["x"].wait()
    x = xe[pl.ds(0, NODE), :]
    near_src[...] = t_dot(own_near[...], x).astype(BF).reshape(6, 16, D)
    far_src[...] = t_dot(own_far[...], x).reshape(FAR, 1, D)

    spot = lax.broadcasted_iota(jnp.int32, (1, EDGE), 1)
    live = spot < count_ref[...]
    s_row = jnp.where(live, sender_ref[...], -1)
    r_row = jnp.where(live, receiver_ref[...] + EXT, -1)
    cols = columns([s_row.astype(F32), r_row.astype(F32)])
    s_col = cols[:, 0:1].astype(jnp.int32)
    r_col = cols[:, 1:2].astype(jnp.int32)
    for k in range(TABLE // 128):
        ids = lax.broadcasted_iota(jnp.int32, (EDGE, 128), 1) + k * 128
        which = s_col if k < EXT // 128 else r_col
        onehot[:, pl.ds(k * 128, 128)] = jnp.where(ids == which, 1.0, 0.0).astype(BF)
    for k in range(TABLE // 128):
        ids = lax.broadcasted_iota(jnp.int32, (128, EDGE), 0) + k * 128
        which = s_row if k < EXT // 128 else r_row
        onehot_t[pl.ds(k * 128, 128), :] = jnp.where(ids == which, 1.0, 0.0).astype(BF)

    pl.semaphore_wait(barrier, 66)

    nears = []
    for k, o in enumerate(OFFSETS):
        one = pltpu.make_async_remote_copy(
            src_ref=near_src.at[k], dst_ref=near_got.at[k],
            send_sem=near_send.at[k], recv_sem=near_recv.at[k],
            device_id=patch_id((me + o + 64) % 64), device_id_type=MESH,
        )
        one.start()
        nears.append(one)

    def far_copy(src, dst, send, recv, d):
        to = (me + d) % 64
        return pltpu.make_async_remote_copy(
            src_ref=src.at[to], dst_ref=dst.at[me], send_sem=send, recv_sem=recv,
            device_id=patch_id(to), device_id_type=MESH,
        )

    @pl.loop(1, 64)
    def _(d):
        far_copy(far_src, far_got, far_send.at[0], far_recv.at[0], d).start()

    def far_wait(src, dst, send, recv):
        all_of = pltpu.make_async_remote_copy(
            src_ref=src.at[pl.ds(0, 63)], dst_ref=dst.at[pl.ds(0, 63)],
            send_sem=send, recv_sem=recv,
            device_id=patch_id((me + 1) % 64), device_id_type=MESH,
        )
        return all_of

    loads["we_in"].wait()
    proj[pl.ds(0, NODE), :] = dot(x, we_in[pl.ds(0, D), :]).astype(BF)
    proj[pl.ds(EXT, NODE), :] = dot(x, we_in[pl.ds(D, D), :]).astype(BF)
    loads["e"].wait()
    pre[...] = dot(e[...], we_in[pl.ds(2 * D, D), :])

    for one in nears:
        one.wait_recv()
    far_all = far_wait(far_src, far_got, far_send.at[0], far_recv.at[0])
    far_all.wait_recv()
    xe[pl.ds(NODE, NEAR), :] = near_got[...].reshape(NEAR, D)
    slot = lax.broadcasted_iota(jnp.int32, (FAR, 1), 0)
    far_rows = jnp.where(slot == me, far_src[...].reshape(FAR, D), far_got[...].reshape(FAR, D))
    xe[pl.ds(NODE + NEAR, FAR), :] = far_rows.astype(BF)
    xe[pl.ds(NODE + NEAR + FAR, 96), :] = jnp.zeros((96, D), BF)
    proj[pl.ds(NODE, EXT - NODE), :] = dot(
        xe[pl.ds(NODE, EXT - NODE), :], we_in[pl.ds(0, D), :]
    ).astype(BF)

    loads["we_out"].wait()

    @pl.loop(0, EDGE // TILE)
    def _(k):
        at = pl.ds(pl.multiple_of(k * TILE, TILE), TILE)
        v = pre[at, :] + dot(onehot[at, :], proj[...])
        s = jax.nn.sigmoid(v)
        h = (v * s).astype(BF)
        hid[at, :] = h
        slope[at, :] = s * (1.0 + v * (1.0 - s))
        normed, inverse = normalize(dot(h, we_out[...]))
        msg[at, :] = normed.astype(BF)
        inv[at, :] = jnp.broadcast_to(inverse, (TILE, 128))

    aggregate = dot(onehot_t[pl.ds(EXT, NODE), :], msg[...]).astype(BF)

    loads["wn_in"].wait()
    node_pre = dot(x, wn_in[pl.ds(0, D), :]) + dot(aggregate, wn_in[pl.ds(D, D), :])
    s = jax.nn.sigmoid(node_pre)
    node_hidden = (node_pre * s).astype(BF)
    node_slope = s * (1.0 + node_pre * (1.0 - s))
    loads["wn_out"].wait()
    node_normed, node_inverse = normalize(dot(node_hidden, wn_out[...]))
    updated = (x.astype(F32) + node_normed).astype(BF)
    loads["wr"].wait()
    predicted = dot(updated, wr[...])
    latitude = -0.5 * jnp.pi + (lat_ref[...].astype(F32) + 0.5) * (jnp.pi / BANDS)
    cols = columns([jnp.cos(latitude), land_ref[...].astype(F32)])
    area, land = cols[:, 0:1], cols[:, 1:2]
    channel = lax.broadcasted_iota(jnp.int32, (NODE, 128), 1)
    weight = jnp.where((channel < OCEAN) & (land == 1.0), 0.0, area)
    loads["t"].wait()
    pred_grad = (weight * (predicted - tgt[...].astype(F32))).astype(BF)
    updated_grad = dot_t(pred_grad, wr[...])
    node_z_grad = norm_back(updated_grad, node_normed, node_inverse).astype(BF)
    node_pre_grad = (dot_t(node_z_grad, wn_out[...]) * node_slope).astype(BF)
    total[...] = updated_grad + dot_t(node_pre_grad, wn_in[pl.ds(0, D), :])
    agg_grad[...] = dot_t(node_pre_grad, wn_in[pl.ds(D, D), :]).astype(BF)

    where = (ix, iy, iz, ic)
    ga, gb = Reducer(group_a, where), Reducer(group_b, where)

    def pack_rows(start0, value, blocks, slots):
        rows = value.reshape(4, 8, 2, blocks, 8, D)
        for b, (h, t) in enumerate(slots):
            for c in range(2):
                for y in range(4):
                    tile = rows[:, :, c, b, :, y * 128 : (y + 1) * 128].astype(BF)
                    start0[h, c, :, y, :, t] = tile

    wgrad[pl.ds(0, D), :] = t_dot(x, node_pre_grad)
    wgrad[pl.ds(D, D), :] = t_dot(aggregate, node_pre_grad)
    pack_rows(ga.start0, wgrad[pl.ds(0, 2 * D), :], 2, ((0, 0), (0, 1)))
    pack_rows(ga.start0, t_dot(node_hidden, node_z_grad), 1, ((1, 0),))
    readout = t_dot(updated, pred_grad).reshape(4, 8, 2, 8, 128)
    for c in range(2):
        for y in range(4):
            ga.start0[1, c, :, y, :, 1] = readout[:, :, c].astype(BF)
    ga.pair()

    @pl.loop(0, EDGE // TILE)
    def _(k):
        at = pl.ds(pl.multiple_of(k * TILE, TILE), TILE)
        g = dot(onehot[at, pl.ds(EXT, NODE)], agg_grad[...])
        z_grad = norm_back(g, msg[at, :].astype(F32), inv[at, :][:, 0:1]).astype(BF)
        ezg[at, :] = z_grad
        epg[at, :] = (dot_t(z_grad, we_out[...]) * slope[at, :]).astype(BF)

    ga.first()
    gsum[...] = dot(onehot_t[...], epg[...]).astype(BF)

    back = dot_t(gsum[pl.ds(NODE, EXT - NODE), :], we_in[pl.ds(0, D), :])
    back_near_src[...] = back[0:NEAR].astype(BF).reshape(6, 16, D)
    back_far_src[...] = back[NEAR : NEAR + FAR].reshape(FAR, 1, D)
    backs = []
    for k, o in enumerate(OFFSETS):
        one = pltpu.make_async_remote_copy(
            src_ref=back_near_src.at[k], dst_ref=back_near_got.at[k],
            send_sem=bnear_send.at[k], recv_sem=bnear_recv.at[k],
            device_id=patch_id((me - o + 64) % 64), device_id_type=MESH,
        )
        one.start()
        backs.append(one)

    @pl.loop(1, 64)
    def _(d):
        far_copy(back_far_src, back_far_got, bfar_send.at[0], bfar_recv.at[0], d).start()

    wgrad[pl.ds(0, D), :] = t_dot(xe[...], gsum[pl.ds(0, EXT), :])
    wgrad[pl.ds(D, D), :] = t_dot(x, gsum[pl.ds(EXT, NODE), :])
    wgrad[pl.ds(2 * D, D), :] = t_dot(e[...], epg[...])
    pack_rows(gb.start0, wgrad[...], 3, ((0, 0), (0, 1), (1, 0)))
    pack_rows(gb.start0, t_dot(hid[...], ezg[...]), 1, ((1, 1),))
    gb.pair()
    ga.second()

    edge_res[...] = dot_t(epg[...], we_in[pl.ds(2 * D, D), :]).astype(BF)
    edge_copy = pltpu.make_async_copy(edge_res, edge_out.at[0], out_sem.at[0])
    edge_copy.start()
    gb.first()
    total[...] += dot_t(gsum[pl.ds(0, NODE), :], we_in[pl.ds(0, D), :]) + dot_t(
        gsum[pl.ds(EXT, NODE), :], we_in[pl.ds(D, D), :]
    )
    ga.third()
    gb.second()
    ga.fourth()

    for one in backs:
        one.wait_recv()
    back_all = far_wait(back_far_src, back_far_got, bfar_send.at[0], bfar_recv.at[0])
    back_all.wait_recv()
    far_rows = jnp.where(
        slot == me, back_far_src[...].reshape(FAR, D), back_far_got[...].reshape(FAR, D)
    ).astype(BF)
    owned = dot(own_near[...], back_near_got[...].reshape(NEAR, D)) + dot(own_far[...], far_rows)
    node_out[0] = (total[...] + owned).astype(BF)

    gb.third()
    parts = ga.last()
    for y in range(4):
        at = pl.ds(y * 128, 128)
        gni_out[pl.ds(0, 8), at] = parts[y][0, 0]
        gni_out[pl.ds(8, 8), at] = parts[y][0, 1]
        gno_out[:, at] = parts[y][1, 0]
    gr_out[...] = parts[0][1, 1]
    gb.fourth()
    parts = gb.last()
    for y in range(4):
        at = pl.ds(y * 128, 128)
        gei_out[pl.ds(0, 8), at] = parts[y][0, 0]
        gei_out[pl.ds(8, 8), at] = parts[y][0, 1]
        gei_out[pl.ds(16, 8), at] = parts[y][1, 0]
        geo_out[:, at] = parts[y][1, 1]

    edge_copy.wait()
    for one in nears + backs:
        one.wait_send()
    far_all.wait_send()
    back_all.wait_send()
    ga.finish()
    gb.finish()


def group_scratch():
    tail = (8, 128)
    return [
        pltpu.VMEM((2, 2, 4, 4, 8, 2, *tail), BF),
        pltpu.VMEM((2, 4, 4, 8, 2, *tail), BF),
        pltpu.VMEM((2, 4, 4, 8, 2, *tail), BF),
        pltpu.VMEM((2, 3, 4, 8, 2, *tail), BF),
        pltpu.VMEM((2, 4, 8, 2, *tail), BF),
        pltpu.VMEM((2, 3, 8, 2, *tail), BF),
        pltpu.VMEM((8, 2, 2, *tail), BF),
        pltpu.VMEM((7, 2, 2, *tail), BF),
        pltpu.VMEM((2, 2, *tail), F32),
        pltpu.VMEM((3, 2, 2, *tail), F32),
        pltpu.SemaphoreType.DMA((24,)),
        pltpu.SemaphoreType.DMA((24,)),
    ]


def body(*args):
    (x, e, t, we_in, we_out, wn_in, wn_out, wr, send, far, sender, receiver, count, land, lat) = args
    anywhere = pl.BlockSpec(memory_space=pl.ANY)
    vmem = pl.BlockSpec(memory_space=pltpu.VMEM)
    near = pltpu.VMEM((6, 16, D), BF)
    row = pltpu.VMEM((FAR, 1, D), F32)
    sem = pltpu.SemaphoreType.DMA
    scratch = [
        pltpu.VMEM((EXT, D), BF),
        pltpu.VMEM((EDGE, D), BF),
        pltpu.VMEM((NODE, 128), BF),
        pltpu.VMEM((3 * D, D), BF),
        pltpu.VMEM((D, D), BF),
        pltpu.VMEM((2 * D, D), BF),
        pltpu.VMEM((D, D), BF),
        pltpu.VMEM((D, 128), BF),
        pltpu.VMEM((EDGE, D), BF),
        near, near, row, row, near, near, row, row,
        pltpu.VMEM((EDGE, TABLE), BF),
        pltpu.VMEM((TABLE, EDGE), BF),
        pltpu.VMEM((NODE, NEAR), BF),
        pltpu.VMEM((NODE, FAR), BF),
        pltpu.VMEM((TABLE, D), BF),
        pltpu.VMEM((EDGE, D), F32),
        pltpu.VMEM((EDGE, D), BF),
        pltpu.VMEM((EDGE, D), F32),
        pltpu.VMEM((EDGE, D), BF),
        pltpu.VMEM((EDGE, 128), F32),
        pltpu.VMEM((EDGE, D), BF),
        pltpu.VMEM((EDGE, D), BF),
        pltpu.VMEM((NODE, D), F32),
        pltpu.VMEM((NODE, D), BF),
        pltpu.VMEM((TABLE, D), BF),
        pltpu.VMEM((3 * D, D), F32),
        sem((8,)), sem((1,)),
        sem((6,)), sem((6,)), sem((1,)), sem((1,)),
        sem((6,)), sem((6,)), sem((1,)), sem((1,)),
    ] + group_scratch() + group_scratch()
    return pl.pallas_call(
        kernel,
        out_shape=(
            jax.ShapeDtypeStruct((1, NODE, D), BF),
            jax.ShapeDtypeStruct((1, EDGE, D), BF),
            jax.ShapeDtypeStruct((24, D), F32),
            jax.ShapeDtypeStruct((8, D), F32),
            jax.ShapeDtypeStruct((16, D), F32),
            jax.ShapeDtypeStruct((8, D), F32),
            jax.ShapeDtypeStruct((8, 128), F32),
        ),
        in_specs=[anywhere] * 8 + [vmem] * 7,
        out_specs=(vmem, anywhere, vmem, vmem, vmem, vmem, vmem),
        scratch_shapes=scratch,
        compiler_params=pltpu.CompilerParams(
            collective_id=0, has_side_effects=True, vmem_limit_bytes=62 * 1024 * 1024
        ),
    )(
        x, e, t, we_in, we_out, wn_in, wn_out, wr, send, far,
        sender.reshape(1, EDGE), receiver.reshape(1, EDGE), count.reshape(1, 1),
        land.reshape(1, NODE), lat.reshape(1, NODE),
    )


def solution(mesh):
    split = Mesh(
        mesh.devices.reshape(4, 8, 2, mesh.shape["rep"]), ("patch_0", "patch_1", "patch_2", "rep")
    )
    in_specs = (
        P("rep", PATCH, None),
        P("rep", PATCH, None),
        P("rep", PATCH, None),
        P(),
        P(),
        P(),
        P(),
        P(),
        P(PATCH, None),
        P(PATCH, None),
        P(PATCH),
        P(PATCH),
        P(PATCH),
        P(PATCH),
        P(PATCH),
    )
    out_specs = (
        P("rep", PATCH, None),
        P("rep", PATCH, None),
        P(PATCH, None),
        P(PATCH, None),
        P(PATCH, None),
        P(PATCH, None),
        P(PATCH, None),
    )
    return jax.shard_map(body, mesh=split, in_specs=in_specs, out_specs=out_specs, check_vma=False)
```

profile of v0, /device:TPU:8, one launch (start us, length us, event | category | flops | bytes accessed | tf_op | source)
XLA Modules:
  0.0 80.0 jit_solution(11446209278651744110)
XLA Ops:
  1.3 1.2 %reshape.32.land_ref = s32[1,384]{1,0:T(1,128)} reshape(s32[384]{0:T(512)} %param.28) | data formatting | bytes 3072 | tf_op jit(solution)/shard_map/reshape | solution.py:520
  2.5 1.2 %reshape.33.lat_ref = s32[1,384]{1,0:T(1,128)} reshape(s32[384]{0:T(512)} %param.29) | data formatting | bytes 3072 | tf_op jit(solution)/shard_map/reshape | solution.py:520
  3.8 1.3 %reshape.29.sender_ref = s32[1,1280]{1,0:T(1,128)} reshape(s32[1280]{0:T(1024)} %param.25) | data formatting | bytes 10240 | tf_op jit(solution)/shard_map/reshape | solution.py:519
  5.1 1.3 %reshape.30.receiver_ref = s32[1,1280]{1,0:T(1,128)} reshape(s32[1280]{0:T(1024)} %param.26) | data formatting | bytes 10240 | tf_op jit(solution)/shard_map/reshape | solution.py:519
  6.4 66.3 %shard_map.198 = (bf16[1,384,512]{2,1,0:T(8,128)(2,1)}, bf16[1,1280,512]{2,1,0:T(8,128)(2,1)}, f32[24,512]{1,0:T(8,128)}, f32[8,512]{1,0:T(8,128)}, f32[16,512]{...) custom-call(bf16[1,384,512]{2,1,0:T(8,128)(2,1)} %x_hbm.1, bf16[1,1280,512]{2,1,0:T(8,128)(2,1)} %e_hbm.1, ...), custom_call_target="tpu_custom_call" | custom-call | tf_op jit(solution)/shard_map/pallas_call | solution.py:500
  72.7 1.8 %copy.30 = bf16[1,384,512]{2,1,0:T(8,128)(2,1)} copy(bf16[1,384,512]{2,1,0:T(8,128)(2,1)} %get-tuple-element.14) | data formatting | bytes 786432
  74.5 0.0 copy-start
  74.5 0.0 copy-start.3
  74.5 0.0 copy-start.1
  74.5 0.0 copy-start.2
  74.5 0.0 copy-start.4
  74.5 2.5 %copy.31 = bf16[1,1280,512]{2,1,0:T(8,128)(2,1)} copy(bf16[1,1280,512]{2,1,0:T(8,128)(2,1)} %get-tuple-element.15) | data formatting | bytes 2621440
  77.0 0.0 copy-done
  77.0 0.6 copy.32
  77.6 0.0 copy-done.3
  77.6 0.6 copy.33
  78.2 0.0 copy-done.1
  78.2 0.6 copy.34
  78.8 0.0 copy-done.2
  78.8 0.6 copy.35
  79.4 0.0 copy-done.4
  79.4 0.6 copy.36
Async XLA Ops:
  74.5 2.5 %copy-start = (f32[24,512]{1,0:T(8,128)S(1)}, f32[24,512]{1,0:T(8,128)}, u32[]{:S(2)}) copy-start(f32[24,512]{1,0:T(8,128)} %get-tuple-element.16) | copy-start | bytes 147460
  74.5 3.1 %copy-start.3 = (f32[8,512]{1,0:T(8,128)S(1)}, f32[8,512]{1,0:T(8,128)}, u32[]{:S(2)}) copy-start(f32[8,512]{1,0:T(8,128)} %get-tuple-element.17) | copy-start | bytes 49156
  74.5 3.8 %copy-start.1 = (f32[16,512]{1,0:T(8,128)S(1)}, f32[16,512]{1,0:T(8,128)}, u32[]{:S(2)}) copy-start(f32[16,512]{1,0:T(8,128)} %get-tuple-element.18) | copy-start | bytes 98308
  74.5 4.4 %copy-start.2 = (f32[8,512]{1,0:T(8,128)S(1)}, f32[8,512]{1,0:T(8,128)}, u32[]{:S(2)}) copy-start(f32[8,512]{1,0:T(8,128)} %get-tuple-element.19) | copy-start | bytes 49156
  74.5 5.0 %copy-start.4 = (f32[8,128]{1,0:T(8,128)S(1)}, f32[8,128]{1,0:T(8,128)}, u32[]{:S(2)}) copy-start(f32[8,128]{1,0:T(8,128)} %get-tuple-element.20) | copy-start | bytes 12292
where the time goes:
time: 80.6 us; the launch traced here: 80 us
  Pallas kernels  66.3 us (82%)
  local copies, waits for them, and re-layouts  12.4 us (15%)
  between operations  1.31 us (2%)
    pallas_call x1, Pallas kernels, body(): pl.pallas_call(kernel, out_shape=(jax.ShapeDtypeStruct((1, NODE, D), BF),...  66.3 us
    unnamed x17, local copies, waits for them, and re-layouts  7.33 us

commit v1 on v0

v1 whole, which is shorter than its diff:
```python
import functools

import jax
import jax.numpy as jnp
from jax import lax
from jax.experimental import pallas as pl
from jax.experimental.pallas import tpu as pltpu
from jax.sharding import Mesh
from jax.sharding import PartitionSpec as P

OCEAN = 32
BANDS = 721
PATCH = ("patch_0", "patch_1", "patch_2")
MESH = pl.DeviceIdType.MESH
D = 512
NODE = 384
EDGE = 1280
NEAR = 96
FAR = 64
EXT = 640
GOT = EXT - NODE
TABLE = EXT + NODE
TILE = 256
OFFSETS = (1, -1, 2, -2, 3, -3)
BF = jnp.bfloat16
F32 = jnp.float32


def dot(a, b):
    return jnp.dot(a, b, preferred_element_type=F32)


def dot_t(a, b):
    return lax.dot_general(a, b, (((1,), (1,)), ((), ())), preferred_element_type=F32)


def t_dot(a, b):
    return lax.dot_general(a, b, (((0,), (0,)), ((), ())), preferred_element_type=F32)


def patch_id(q):
    return {"patch_0": q // 16, "patch_1": (q // 2) % 8, "patch_2": q % 2}


def greet(barrier, device):
    pl.semaphore_signal(barrier, inc=1, device_id=device, device_id_type=MESH)


def normalize(v):
    mean = jnp.mean(v, axis=-1, keepdims=True)
    centred = v - mean
    var = jnp.mean(centred * centred, axis=-1, keepdims=True)
    inverse = lax.rsqrt(var + 1e-05)
    return centred * inverse, inverse


def norm_back(g, y, inverse):
    first = jnp.mean(g, axis=-1, keepdims=True)
    second = jnp.mean(g * y, axis=-1, keepdims=True)
    return inverse * (g - first - y * second)


def columns(rows):
    wide = rows[0].shape[1]
    pad = [jnp.zeros((8 - len(rows), wide), F32)]
    return jnp.concatenate(rows + pad, axis=0).T


class Reducer:
    def __init__(self, refs, where):
        (self.start0, self.r0, self.w1, self.direct, self.relay, self.merged, self.carried,
         self.w2, self.r2, self.w3, self.r3, self.w4, self.r4, self.send, self.recv) = refs
        x, self.y, self.z, self.c = where
        self.axes = ((("patch_0", x), ("rep", self.y)), (("rep", self.y), ("patch_0", x)))
        self.pending = []

    def copy(self, src, dst, k, device):
        one = pltpu.make_async_remote_copy(
            src_ref=src, dst_ref=dst, send_sem=self.send.at[k], recv_sem=self.recv.at[k],
            device_id=device, device_id_type=MESH,
        )
        one.start()
        self.pending.append(one)
        return one

    def pair(self):
        other = 1 - self.c
        self.c0 = [
            self.copy(self.start0.at[h, other], self.r0.at[h], h, {"patch_2": other})
            for h in range(2)
        ]

    def first(self):
        self.c1 = []
        for h in range(2):
            self.c0[h].wait_recv()

            @pl.loop(0, 4)
            def _(i):
                mine = self.start0[h, self.c, i].astype(F32)
                self.w1[h, i] = (mine + self.r0[h, i].astype(F32)).astype(BF)

            axis, at = self.axes[h][0]
            right, left, across = (at + 1) % 4, (at + 3) % 4, (at + 2) % 4
            lo, hi = pl.ds(0, 2), pl.ds(2, 2)
            w1, k = self.w1, 2 + 6 * h
            self.c1.append((
                self.copy(w1.at[h, across, lo], self.relay.at[h, 0], k, {axis: right}),
                self.copy(w1.at[h, across, hi], self.relay.at[h, 1], k + 1, {axis: left}),
                self.copy(w1.at[h, left, lo], self.direct.at[h, 0], k + 2, {axis: left}),
                self.copy(w1.at[h, right, hi], self.direct.at[h, 1], k + 3, {axis: right}),
            ))

    def middle(self):
        self.c1b = []
        for h in range(2):
            axis, at = self.axes[h][0]
            ends = ((at + 1) % 4, (at + 3) % 4)
            for side in range(2):
                self.c1[h][side].wait_recv()
                mine = self.w1[h, ends[side], pl.ds(2 * side, 2)].astype(F32)
                self.merged[h, side] = (mine + self.relay[h, side].astype(F32)).astype(BF)
                self.c1b.append(self.copy(
                    self.merged.at[h, side], self.carried.at[h, side], 6 + 6 * h + side,
                    {axis: ends[side]},
                ))

    def second(self):
        self.c2 = []
        for h in range(2):
            _, own = self.axes[h][0]
            for side in range(2):
                self.c1[h][2 + side].wait_recv()
                self.c1b[2 * h + side].wait_recv()
                part = pl.ds(2 * side, 2)
                acc = self.w1[h, own, part].astype(F32) + self.direct[h, side].astype(F32)
                self.w2[h, part] = (acc + self.carried[h, side].astype(F32)).astype(BF)
            axis, at = self.axes[h][1]
            for d in range(1, 4):
                to = (at + d) % 4
                self.c2.append(
                    self.copy(self.w2.at[h, to], self.r2.at[h, d - 1], 13 + 3 * h + d, {axis: to})
                )

    def third(self):
        for h in range(2):
            for one in self.c2[3 * h : 3 * h + 3]:
                one.wait_recv()
            acc = self.w2[h, self.axes[h][1][1]].astype(F32)
            for s in range(3):
                acc = acc + self.r2[h, s].astype(F32)
            self.w3[:, h] = acc.astype(BF)
        self.c3 = []
        for d in range(1, 8):
            to = (self.z + d) % 8
            self.c3.append(self.copy(self.w3.at[to], self.r3.at[d - 1], 19 + d, {"patch_1": to}))

    def fourth(self):
        for one in self.c3:
            one.wait_recv()
        acc = self.w3[self.z].astype(F32)
        for s in range(7):
            acc = acc + self.r3[s].astype(F32)
        self.w4[...] = acc * (1.0 / (NODE * 64 * 4))
        self.c4 = []
        for d in range(1, 4):
            to = (self.y + d) % 4
            self.c4.append(self.copy(self.w4, self.r4.at[d - 1], 26 + d, {"rep": to}))

    def last(self):
        for one in self.c4:
            one.wait_recv()
        out = []
        own = self.w4[...]
        got = [self.r4[s] for s in range(3)]
        for y in range(4):
            tile = own
            for s in range(3):
                tile = jnp.where((self.y - s - 1 + 4) % 4 == y, got[s], tile)
            out.append(tile)
        return out

    def finish(self):
        for one in self.pending:
            one.wait_send()


def kernel(
    x_hbm, e_hbm, t_hbm, we_in_hbm, we_out_hbm, wn_in_hbm, wn_out_hbm, wr_hbm,
    send_hbm, far_hbm, sender_hbm, receiver_hbm, count_ref, land_hbm, lat_hbm,
    node_out, edge_out, grads_out,
    send_ref, far_ref, sender_ref, receiver_ref, land_ref, lat_ref,
    xe, e, tgt, we_in, we_out, wn_in, wn_out, wr, edge_res,
    near_src, near_got, far_src, far_got, back_near_src, back_near_got, back_far_src, back_far_mid, back_far_got,
    onehot, onehot_t, own_near, own_far, proj, pre, hid, msg, inv, ezg, epg, total, agg_grad, gsum, wgrad, node_res, grads,
    *rest,
):
    dma_sem, out_sem, near_send, near_recv, far_send, far_recv = rest[:6]
    bnear_send, bnear_recv, bfar_send, bfar_recv = rest[6:10]
    group_a, group_b = rest[10:25], rest[25:40]
    ix, iz, ic, iy = (lax.axis_index(a) for a in (*PATCH, "rep"))
    me = ix * 16 + iz * 2 + ic

    loads = {}
    for k, (name, src, dst) in enumerate((
        ("send", send_hbm, send_ref),
        ("far", far_hbm, far_ref),
        ("sender", sender_hbm, sender_ref),
        ("receiver", receiver_hbm, receiver_ref),
        ("x", x_hbm.at[0], xe.at[pl.ds(GOT, NODE)]),
        ("we_in", we_in_hbm, we_in),
        ("e", e_hbm.at[0], e),
        ("we_out", we_out_hbm, we_out),
        ("wn_in", wn_in_hbm, wn_in),
        ("wn_out", wn_out_hbm, wn_out),
        ("wr", wr_hbm, wr),
        ("t", t_hbm.at[0], tgt),
        ("land", land_hbm, land_ref),
        ("lat", lat_hbm, lat_ref),
    )):
        loads[name] = pltpu.make_async_copy(src, dst, dma_sem.at[k])
        loads[name].start()

    barrier = pltpu.get_barrier_semaphore()

    @pl.loop(0, 63, unroll=7)
    def _(k):
        greet(barrier, patch_id((me + 1 + (k + 32) % 63) % 64))

    for d in range(1, 4):
        greet(barrier, {"rep": (iy + d) % 4})

    loads["send"].wait()
    loads["far"].wait()
    ids = lax.broadcasted_iota(jnp.int32, (NODE, NEAR), 0)
    own_near[...] = jnp.where(ids == send_ref[...], 1.0, 0.0).astype(BF)
    ids = lax.broadcasted_iota(jnp.int32, (NODE, FAR), 0)
    own_far[...] = jnp.where(ids == far_ref[...], 1.0, 0.0).astype(BF)
    loads["x"].wait()
    x = xe[pl.ds(GOT, NODE), :]
    near_src[...] = t_dot(own_near[...], x).astype(BF).reshape(6, 16, D)
    far_src[...] = t_dot(own_far[...], x).astype(BF).reshape(FAR, 4, 128)

    pl.semaphore_wait(barrier, 66)

    nears = []
    for k, o in enumerate(OFFSETS):
        one = pltpu.make_async_remote_copy(
            src_ref=near_src.at[k], dst_ref=near_got.at[k],
            send_sem=near_send.at[k], recv_sem=near_recv.at[k],
            device_id=patch_id((me + o + 64) % 64), device_id_type=MESH,
        )
        one.start()
        nears.append(one)

    def remote(src, dst, sems, k, device):
        one = pltpu.make_async_remote_copy(
            src_ref=src, dst_ref=dst, send_sem=sems[0].at[k], recv_sem=sems[1].at[k],
            device_id=device, device_id_type=MESH,
        )
        one.start()
        return one

    def plane(k):
        return {"patch_0": k // 2, "patch_2": k % 2}

    @pl.loop(0, 63, unroll=7)
    def _(k):
        to = (me + 1 + (k + 32) % 63) % 64
        pltpu.make_async_remote_copy(
            src_ref=far_src.at[to], dst_ref=far_got.at[me],
            send_sem=far_send.at[0], recv_sem=far_recv.at[0],
            device_id=patch_id(to), device_id_type=MESH,
        ).start()

    far_all = pltpu.make_async_remote_copy(
        src_ref=far_src.at[pl.ds(0, 63)], dst_ref=far_got.at[pl.ds(0, 63)],
        send_sem=far_send.at[0], recv_sem=far_recv.at[0],
        device_id=patch_id((me + 1) % 64), device_id_type=MESH,
    )

    spot = lax.broadcasted_iota(jnp.int32, (1, EDGE), 1)
    live = spot < count_ref[0]
    loads["sender"].wait()
    loads["receiver"].wait()
    s_row = sender_ref[...].reshape(1, EDGE)
    s_row = jnp.where(live, jnp.where(s_row < NODE, s_row + GOT, s_row - NODE), -1)
    r_row = jnp.where(live, receiver_ref[...].reshape(1, EDGE) + EXT, -1)
    cols = columns([s_row.astype(F32), r_row.astype(F32)])
    s_col = cols[:, 0:1].astype(jnp.int32)
    r_col = cols[:, 1:2].astype(jnp.int32)
    for k in range(TABLE // 128):
        ids = lax.broadcasted_iota(jnp.int32, (EDGE, 128), 1) + k * 128
        which = s_col if k < EXT // 128 else r_col
        onehot[:, pl.ds(k * 128, 128)] = jnp.where(ids == which, 1.0, 0.0).astype(BF)
    for k in range(TABLE // 128):
        ids = lax.broadcasted_iota(jnp.int32, (128, EDGE), 0) + k * 128
        which = s_row if k < EXT // 128 else r_row
        onehot_t[pl.ds(k * 128, 128), :] = jnp.where(ids == which, 1.0, 0.0).astype(BF)

    loads["we_in"].wait()
    proj[pl.ds(GOT, NODE), :] = dot(x, we_in[pl.ds(0, D), :]).astype(BF)
    proj[pl.ds(EXT, NODE), :] = dot(x, we_in[pl.ds(D, D), :]).astype(BF)
    loads["e"].wait()
    pre[...] = dot(e[...], we_in[pl.ds(2 * D, D), :]) + dot(
        onehot[:, pl.ds(GOT, 2 * NODE)], proj[pl.ds(GOT, 2 * NODE), :]
    )

    for one in nears:
        one.wait_recv()
    far_all.wait_recv()
    xe[pl.ds(0, NEAR), :] = near_got[...].reshape(NEAR, D)
    slot = lax.broadcasted_iota(jnp.int32, (FAR, 4, 128), 0)
    far_rows = jnp.where(slot == me, far_src[...], far_got[...]).reshape(FAR, D)
    xe[pl.ds(NEAR, FAR), :] = far_rows
    xe[pl.ds(NEAR + FAR, 96), :] = jnp.zeros((96, D), BF)
    proj[pl.ds(0, GOT), :] = dot(xe[pl.ds(0, GOT), :], we_in[pl.ds(0, D), :]).astype(BF)

    loads["we_out"].wait()

    for k in range(EDGE // TILE):
        at = pl.ds(k * TILE, TILE)
        v = pre[at, :] + dot(onehot[at, pl.ds(0, GOT)], proj[pl.ds(0, GOT), :])
        s = jax.nn.sigmoid(v)
        h = (v * s).astype(BF)
        hid[at, :] = h
        pre[at, :] = s * (1.0 + v * (1.0 - s))
        normed, inverse = normalize(dot(h, we_out[...]))
        msg[at, :] = normed.astype(BF)
        inv[at, :] = jnp.broadcast_to(inverse, (TILE, 128))

    aggregate = dot(onehot_t[pl.ds(EXT, NODE), :], msg[...]).astype(BF)

    loads["wn_in"].wait()
    node_pre = dot(x, wn_in[pl.ds(0, D), :]) + dot(aggregate, wn_in[pl.ds(D, D), :])
    s = jax.nn.sigmoid(node_pre)
    node_hidden = (node_pre * s).astype(BF)
    node_slope = s * (1.0 + node_pre * (1.0 - s))
    loads["wn_out"].wait()
    node_normed, node_inverse = normalize(dot(node_hidden, wn_out[...]))
    updated = (x.astype(F32) + node_normed).astype(BF)
    loads["wr"].wait()
    predicted = dot(updated, wr[...])
    loads["land"].wait()
    loads["lat"].wait()
    latitude = -0.5 * jnp.pi + (lat_ref[...].reshape(1, NODE).astype(F32) + 0.5) * (jnp.pi / BANDS)
    cols = columns([jnp.cos(latitude), land_ref[...].reshape(1, NODE).astype(F32)])
    area, land = cols[:, 0:1], cols[:, 1:2]
    channel = lax.broadcasted_iota(jnp.int32, (NODE, 128), 1)
    weight = jnp.where((channel < OCEAN) & (land == 1.0), 0.0, area)
    loads["t"].wait()
    pred_grad = (weight * (predicted - tgt[...].astype(F32))).astype(BF)
    updated_grad = dot_t(pred_grad, wr[...])
    node_z_grad = norm_back(updated_grad, node_normed, node_inverse).astype(BF)
    node_pre_grad = (dot_t(node_z_grad, wn_out[...]) * node_slope).astype(BF)
    total[...] = updated_grad + dot_t(node_pre_grad, wn_in[pl.ds(0, D), :])
    agg_grad[...] = dot_t(node_pre_grad, wn_in[pl.ds(D, D), :]).astype(BF)

    where = (ix, iy, iz, ic)
    ga, gb = Reducer(group_a, where), Reducer(group_b, where)

    def pack_rows(start0, value, blocks, slots):
        rows = value.reshape(4, 8, 2, blocks, 8, D)
        for b, (h, t) in enumerate(slots):
            for c in range(2):
                for y in range(4):
                    tile = rows[:, :, c, b, :, y * 128 : (y + 1) * 128].astype(BF)
                    if h == 0:
                        start0[h, c, :, y, :, t] = tile
                    else:
                        start0[h, c, y, :, :, t] = tile

    wgrad[pl.ds(0, D), :] = t_dot(x, node_pre_grad)
    wgrad[pl.ds(D, D), :] = t_dot(aggregate, node_pre_grad)
    pack_rows(ga.start0, wgrad[pl.ds(0, 2 * D), :], 2, ((0, 0), (0, 1)))
    pack_rows(ga.start0, t_dot(node_hidden, node_z_grad), 1, ((1, 0),))
    readout = t_dot(updated, pred_grad).reshape(4, 8, 2, 8, 128)
    for c in range(2):
        for y in range(4):
            ga.start0[1, c, y, :, :, 1] = readout[:, :, c].astype(BF)
    ga.pair()

    def edge_backward(k):
        at = pl.ds(k * TILE, TILE)
        g = dot(onehot[at, pl.ds(EXT, NODE)], agg_grad[...])
        z_grad = norm_back(g, msg[at, :].astype(F32), inv[at, :][:, 0:1]).astype(BF)
        ezg[at, :] = z_grad
        epg[at, :] = (dot_t(z_grad, we_out[...]) * pre[at, :]).astype(BF)

    for k in range(EDGE // TILE):
        edge_backward(k)
        if k == 2:
            ga.first()
    gsum[...] = dot(onehot_t[...], epg[...]).astype(BF)
    ga.middle()

    wgrad[pl.ds(0, D), :] = t_dot(xe[...], gsum[pl.ds(0, EXT), :])
    wgrad[pl.ds(D, D), :] = t_dot(x, gsum[pl.ds(EXT, NODE), :])
    wgrad[pl.ds(2 * D, D), :] = t_dot(e[...], epg[...])
    pack_rows(gb.start0, wgrad[...], 3, ((0, 0), (0, 1), (1, 0)))
    pack_rows(gb.start0, t_dot(hid[...], ezg[...]), 1, ((1, 1),))
    gb.pair()
    back = dot_t(gsum[pl.ds(0, GOT), :], we_in[pl.ds(0, D), :])
    back_near_src[...] = back[0:NEAR].astype(BF).reshape(6, 16, D)
    back_far_src[...] = back[NEAR : NEAR + FAR].astype(BF).reshape(4, 8, 2, 4, 128)
    backs = []
    for k, o in enumerate(OFFSETS):
        one = pltpu.make_async_remote_copy(
            src_ref=back_near_src.at[k], dst_ref=back_near_got.at[k],
            send_sem=bnear_send.at[k], recv_sem=bnear_recv.at[k],
            device_id=patch_id((me - o + 64) % 64), device_id_type=MESH,
        )
        one.start()
        backs.append(one)

    spot_xc = ix * 2 + ic
    bfars = []

    def remote(src, dst, sems, k, device):
        one = pltpu.make_async_remote_copy(
            src_ref=src, dst_ref=dst, send_sem=sems[0].at[k], recv_sem=sems[1].at[k],
            device_id=device, device_id_type=MESH,
        )
        one.start()
        return one

    for d in range(1, 8):
        to = (iz + d) % 8
        bfars.append(remote(
            back_far_src.at[:, to], back_far_mid.at[iz], (bfar_send, bfar_recv), d - 1,
            {"patch_1": to},
        ))
    back_far_mid[pl.ds(iz, 1)] = back_far_src[:, pl.ds(iz, 1)].reshape(1, 4, 2, 4, 128)

    edge_res[...] = dot_t(epg[...], we_in[pl.ds(2 * D, D), :]).astype(BF)
    edge_copy = pltpu.make_async_copy(edge_res, edge_out.at[0], out_sem.at[0])
    edge_copy.start()
    gb.first()
    ga.second()
    total[...] += dot_t(gsum[pl.ds(GOT, NODE), :], we_in[pl.ds(0, D), :]) + dot_t(
        gsum[pl.ds(EXT, NODE), :], we_in[pl.ds(D, D), :]
    )
    gb.middle()

    for one in bfars:
        one.wait_recv()
    for d in range(1, 8):
        to = (spot_xc + d) % 8
        bfars.append(remote(
            back_far_mid.at[:, to // 2, to % 2], back_far_got.at[ix, :, ic],
            (bfar_send, bfar_recv), 6 + d, {"patch_0": to // 2, "patch_2": to % 2},
        ))
    back_far_got[pl.ds(ix, 1), :, pl.ds(ic, 1)] = back_far_mid[
        :, pl.ds(ix, 1), pl.ds(ic, 1)
    ].reshape(1, 8, 1, 4, 128)
    gb.second()
    ga.third()

    for one in backs + bfars[7:]:
        one.wait_recv()
    far_rows = back_far_got[...].reshape(FAR, D)
    owned = dot(own_near[...], back_near_got[...].reshape(NEAR, D)) + dot(own_far[...], far_rows)
    node_res[...] = (total[...] + owned).astype(BF)
    node_copy = pltpu.make_async_copy(node_res, node_out.at[0], out_sem.at[1])
    node_copy.start()

    gb.third()
    ga.fourth()
    gb.fourth()
    parts = ga.last()
    for y in range(4):
        at = pl.ds(y * 128, 128)
        grads[pl.ds(32, 8), at] = parts[y][0, 0]
        grads[pl.ds(40, 8), at] = parts[y][0, 1]
        grads[pl.ds(48, 8), at] = parts[y][1, 0]
    grads[pl.ds(56, 8), pl.ds(0, 128)] = parts[0][1, 1]
    grads[pl.ds(56, 8), pl.ds(128, 384)] = jnp.zeros((8, 384), F32)
    parts = gb.last()
    for y in range(4):
        at = pl.ds(y * 128, 128)
        grads[pl.ds(0, 8), at] = parts[y][0, 0]
        grads[pl.ds(8, 8), at] = parts[y][0, 1]
        grads[pl.ds(16, 8), at] = parts[y][1, 0]
        grads[pl.ds(24, 8), at] = parts[y][1, 1]
    grads_copy = pltpu.make_async_copy(grads, grads_out, dma_sem.at[0])
    grads_copy.start()

    grads_copy.wait()
    node_copy.wait()
    edge_copy.wait()
    for one in nears + backs + bfars:
        one.wait_send()
    far_all.wait_send()
    ga.finish()
    gb.finish()


def hand_out(node, edge, grads, *rest):
    outs, (node_v, edge_v, grads_v, take_sem, give_sem) = rest[:7], rest[7:]
    parts = ((0, 24, D), (24, 8, D), (32, 16, D), (48, 8, D), (56, 8, 128))
    steps = [(grads, grads_v, [
        (grads_v.at[pl.ds(at, n), pl.ds(0, w)], outs[2 + k]) for k, (at, n, w) in enumerate(parts)
    ])]
    for k in range(5):
        at = pl.ds(k * TILE, TILE)
        steps.append((edge.at[0, at], edge_v.at[at], [(edge_v.at[at], outs[1].at[0, at])]))
    steps.append((node.at[0], node_v, [(node_v, outs[0].at[0])]))
    takes, gives = [], []
    for k, (src, dst, _) in enumerate(steps):
        takes.append(pltpu.make_async_copy(src, dst, take_sem.at[k]))
        takes[-1].start()
    for k, (_, _, moves) in enumerate(steps):
        takes[k].wait()
        for src, dst in moves:
            gives.append(pltpu.make_async_copy(src, dst, give_sem.at[len(gives)]))
            gives[-1].start()
    for one in gives:
        one.wait()


def group_scratch():
    tail = (8, 128)
    return [
        pltpu.VMEM((2, 2, 4, 4, 8, 2, *tail), BF),
        pltpu.VMEM((2, 4, 4, 8, 2, *tail), BF),
        pltpu.VMEM((2, 4, 4, 8, 2, *tail), BF),
        pltpu.VMEM((2, 2, 2, 8, 2, *tail), BF),
        pltpu.VMEM((2, 2, 2, 8, 2, *tail), BF),
        pltpu.VMEM((2, 2, 2, 8, 2, *tail), BF),
        pltpu.VMEM((2, 2, 2, 8, 2, *tail), BF),
        pltpu.VMEM((2, 4, 8, 2, *tail), BF),
        pltpu.VMEM((2, 3, 8, 2, *tail), BF),
        pltpu.VMEM((8, 2, 2, *tail), BF),
        pltpu.VMEM((7, 2, 2, *tail), BF),
        pltpu.VMEM((2, 2, *tail), F32),
        pltpu.VMEM((3, 2, 2, *tail), F32),
        pltpu.SemaphoreType.DMA((30,)),
        pltpu.SemaphoreType.DMA((30,)),
    ]


def body(*args):
    (x, e, t, we_in, we_out, wn_in, wn_out, wr, send, far, sender, receiver, count, land, lat) = args
    anywhere = pl.BlockSpec(memory_space=pl.ANY)
    hbm = pl.BlockSpec(memory_space=pltpu.HBM)
    near = pltpu.VMEM((6, 16, D), BF)
    row = pltpu.VMEM((FAR, 4, 128), BF)
    natural = pltpu.VMEM((4, 8, 2, 4, 128), BF)
    turned = pltpu.VMEM((8, 4, 2, 4, 128), BF)
    sem = pltpu.SemaphoreType.DMA
    scratch = [
        pltpu.VMEM((1, NEAR), jnp.int32),
        pltpu.VMEM((1, FAR), jnp.int32),
        pltpu.VMEM((EDGE,), jnp.int32),
        pltpu.VMEM((EDGE,), jnp.int32),
        pltpu.VMEM((NODE,), jnp.int32),
        pltpu.VMEM((NODE,), jnp.int32),
        pltpu.VMEM((EXT, D), BF),
        pltpu.VMEM((EDGE, D), BF),
        pltpu.VMEM((NODE, 128), BF),
        pltpu.VMEM((3 * D, D), BF),
        pltpu.VMEM((D, D), BF),
        pltpu.VMEM((2 * D, D), BF),
        pltpu.VMEM((D, D), BF),
        pltpu.VMEM((D, 128), BF),
        pltpu.VMEM((EDGE, D), BF),
        near, near, row, row, near, near, natural, turned, natural,
        pltpu.VMEM((EDGE, TABLE), BF),
        pltpu.VMEM((TABLE, EDGE), BF),
        pltpu.VMEM((NODE, NEAR), BF),
        pltpu.VMEM((NODE, FAR), BF),
        pltpu.VMEM((TABLE, D), BF),
        pltpu.VMEM((EDGE, D), F32),
        pltpu.VMEM((EDGE, D), BF),
        pltpu.VMEM((EDGE, D), BF),
        pltpu.VMEM((EDGE, 128), F32),
        pltpu.VMEM((EDGE, D), BF),
        pltpu.VMEM((EDGE, D), BF),
        pltpu.VMEM((NODE, D), F32),
        pltpu.VMEM((NODE, D), BF),
        pltpu.VMEM((TABLE, D), BF),
        pltpu.VMEM((3 * D, D), F32),
        pltpu.VMEM((NODE, D), BF),
        pltpu.VMEM((64, D), F32),
        sem((14,)), sem((2,)),
        sem((6,)), sem((6,)), sem((1,)), sem((1,)),
        sem((6,)), sem((6,)), sem((14,)), sem((14,)),
    ] + group_scratch() + group_scratch()
    shapes = (
        jax.ShapeDtypeStruct((1, NODE, D), BF),
        jax.ShapeDtypeStruct((1, EDGE, D), BF),
        jax.ShapeDtypeStruct((24, D), F32),
        jax.ShapeDtypeStruct((8, D), F32),
        jax.ShapeDtypeStruct((16, D), F32),
        jax.ShapeDtypeStruct((8, D), F32),
        jax.ShapeDtypeStruct((8, 128), F32),
    )
    results = pl.pallas_call(
        kernel,
        out_shape=(*shapes[:2], jax.ShapeDtypeStruct((64, D), F32)),
        in_specs=[hbm] * 12 + [pl.BlockSpec(memory_space=pltpu.SMEM)] + [hbm] * 2,
        out_specs=(anywhere,) * 3,
        scratch_shapes=scratch,
        compiler_params=pltpu.CompilerParams(
            collective_id=0, has_side_effects=True, vmem_limit_bytes=62 * 1024 * 1024
        ),
    )(
        x, e, t, we_in, we_out, wn_in, wn_out, wr, send, far,
        sender, receiver, count, land, lat,
    )
    return pl.pallas_call(
        hand_out,
        out_shape=shapes,
        in_specs=[anywhere] * 3,
        out_specs=(hbm,) * 7,
        scratch_shapes=[
            pltpu.VMEM((NODE, D), BF),
            pltpu.VMEM((EDGE, D), BF),
            pltpu.VMEM((64, D), F32),
            sem((7,)),
            sem((11,)),
        ],
        compiler_params=pltpu.CompilerParams(vmem_limit_bytes=60 * 1024 * 1024),
    )(*results)


def solution(mesh):
    split = Mesh(
        mesh.devices.reshape(4, 8, 2, mesh.shape["rep"]), ("patch_0", "patch_1", "patch_2", "rep")
    )
    in_specs = (
        P("rep", PATCH, None),
        P("rep", PATCH, None),
        P("rep", PATCH, None),
        P(),
        P(),
        P(),
        P(),
        P(),
        P(PATCH, None),
        P(PATCH, None),
        P(PATCH),
        P(PATCH),
        P(PATCH),
        P(PATCH),
        P(PATCH),
    )
    out_specs = (
        P("rep", PATCH, None),
        P("rep", PATCH, None),
        P(PATCH, None),
        P(PATCH, None),
        P(PATCH, None),
        P(PATCH, None),
        P(PATCH, None),
    )
    return jax.shard_map(body, mesh=split, in_specs=in_specs, out_specs=out_specs, check_vma=False)
```

time: 80.6 us -> 65.6 us (0.81)
  local copies, waits for them, and re-layouts: 12.4 us -> 0 us
  Pallas kernels: 66.3 us -> 64 us
    unnamed x17 -> x0, local copies, waits for them, and re-layouts: 7.33 us -> none
    reshape x4 -> x0, local copies, waits for them, and re-layouts: 5.08 us -> none  [the longest x1 1.29 us: body(): sender.reshape(1, EDGE)]
    pallas_call x1 -> x2, Pallas kernels: 66.3 us -> 64 us  [the longest x1 61.7 us: body(): pl.pallas_call(kernel, out_shape=(*shapes[:2], jax.ShapeDtypeStruct((64,...]
where the time goes in v1:
time: 65.6 us; the launch traced here: 65.5 us
  Pallas kernels  64 us (98%)
  between operations  1.45 us (2%)
    pallas_call x1, Pallas kernels, body(): pl.pallas_call(kernel, out_shape=(*shapes[:2], jax.ShapeDtypeStruct((64,...  61.7 us
    pallas_call x1, Pallas kernels, body(): pl.pallas_call(hand_out, out_shape=shapes, in_specs=[anywhere] * 3, out_s...  2.37 us

profile of v1, /device:TPU:8, one launch (start us, length us, event | category | flops | bytes accessed | tf_op | source)
XLA Modules:
  0.0 65.5 jit_solution(2881440705290052582)
XLA Ops:
  1.3 61.7 %shard_map.198 = (bf16[1,384,512]{2,1,0:T(8,128)(2,1)}, bf16[1,1280,512]{2,1,0:T(8,128)(2,1)}, f32[64,512]{1,0:T(8,128)}) custom-call(bf16[1,384,512]{2,1,0:T(8,128)(2,1)} %x_hbm.1, bf16[1,1280,512]{2,1,0:T(8,128)(2,1)} %e_hbm.1, bf16[1,384,128]{2,1,0:T(8,128)(2,1)} %t_hbm.1, bf16[1536,512]{1,0:T(8,128)(2,1)} %we_in_hbm.1, bf16[512,512]{1,0:T(8,128)(2,1)} %we_out_hbm.1, ...), custom_call_target="tpu_custom_call" | custom-call | tf_op jit(solution)/shard_map/pallas_call | solution.py:598
  62.9 2.4 %shard_map.199 = (bf16[1,384,512]{2,1,0:T(8,128)(2,1)}, bf16[1,1280,512]{2,1,0:T(8,128)(2,1)}, f32[24,512]{1,0:T(8,128)}, f32[8,512]{1,0:T(8,128)}, f32[16,512]{...) custom-call(bf16[1,384,512]{2,1,0:T(8,128)(2,1)} %get-tuple-element.10.node, ...), custom_call_target="tpu_custom_call" | custom-call | tf_op jit(solution)/shard_map/pallas_call | solution.py:611

commit v2 on v1

--- a/solution.py
+++ b/solution.py
@@ -190,14 +190,14 @@
     send_hbm, far_hbm, sender_hbm, receiver_hbm, count_ref, land_hbm, lat_hbm,
     node_out, edge_out, grads_out,
     send_ref, far_ref, sender_ref, receiver_ref, land_ref, lat_ref,
-    xe, e, tgt, we_in, we_out, wn_in, wn_out, wr, edge_res,
+    xe, e, tgt, we_in, we_out, wn_in, wn_out, wr,
     near_src, near_got, far_src, far_got, back_near_src, back_near_got, back_far_src, back_far_mid, back_far_got,
-    onehot, onehot_t, own_near, own_far, proj, pre, hid, msg, inv, ezg, epg, total, agg_grad, gsum, wgrad, node_res, grads,
+    onehot, onehot_t, own_near, own_far, proj, pre, hid, msg, inv, ezg, epg, total, agg_grad, gsum, wgrad,
     *rest,
 ):
-    dma_sem, out_sem, near_send, near_recv, far_send, far_recv = rest[:6]
-    bnear_send, bnear_recv, bfar_send, bfar_recv = rest[6:10]
-    group_a, group_b = rest[10:25], rest[25:40]
+    dma_sem, near_send, near_recv, far_send, far_recv = rest[:5]
+    bnear_send, bnear_recv, bfar_send, bfar_recv = rest[5:9]
+    group_a, group_b = rest[9:24], rest[24:39]
     ix, iz, ic, iy = (lax.axis_index(a) for a in (*PATCH, "rep"))
     me = ix * 16 + iz * 2 + ic
 
@@ -223,9 +223,16 @@
 
     barrier = pltpu.get_barrier_semaphore()
 
-    @pl.loop(0, 63, unroll=7)
-    def _(k):
-        greet(barrier, patch_id((me + 1 + (k + 32) % 63) % 64))
+    xs, zs, cs = ([(i + d) % n for d in range(n)] for i, n in ((ix, 4), (iz, 8), (ic, 2)))
+    others = [
+        (dx, dz, dc)
+        for dx in (2, 1, 3, 0)
+        for dz in (4, 3, 5, 2, 6, 1, 7, 0)
+        for dc in range(2)
+        if dx or dz or dc
+    ]
+    for dx, dz, dc in others:
+        greet(barrier, {"patch_0": xs[dx], "patch_1": zs[dz], "patch_2": cs[dc]})
 
     for d in range(1, 4):
         greet(barrier, {"rep": (iy + d) % 4})
@@ -239,7 +246,7 @@
     loads["x"].wait()
     x = xe[pl.ds(GOT, NODE), :]
     near_src[...] = t_dot(own_near[...], x).astype(BF).reshape(6, 16, D)
-    far_src[...] = t_dot(own_far[...], x).astype(BF).reshape(FAR, 4, 128)
+    far_src[...] = t_dot(own_far[...], x).astype(BF).reshape(4, 8, 2, 4, 128)
 
     pl.semaphore_wait(barrier, 66)
 
@@ -264,17 +271,16 @@
     def plane(k):
         return {"patch_0": k // 2, "patch_2": k % 2}
 
-    @pl.loop(0, 63, unroll=7)
-    def _(k):
-        to = (me + 1 + (k + 32) % 63) % 64
+    for dx, dz, dc in others:
         pltpu.make_async_remote_copy(
-            src_ref=far_src.at[to], dst_ref=far_got.at[me],
+            src_ref=far_src.at[xs[dx], zs[dz], cs[dc]], dst_ref=far_got.at[me],
             send_sem=far_send.at[0], recv_sem=far_recv.at[0],
-            device_id=patch_id(to), device_id_type=MESH,
+            device_id={"patch_0": xs[dx], "patch_1": zs[dz], "patch_2": cs[dc]},
+            device_id_type=MESH,
         ).start()
 
     far_all = pltpu.make_async_remote_copy(
-        src_ref=far_src.at[pl.ds(0, 63)], dst_ref=far_got.at[pl.ds(0, 63)],
+        src_ref=far_got.at[pl.ds(0, 63)], dst_ref=far_got.at[pl.ds(0, 63)],
         send_sem=far_send.at[0], recv_sem=far_recv.at[0],
         device_id=patch_id((me + 1) % 64), device_id_type=MESH,
     )
@@ -306,33 +312,50 @@
         onehot[:, pl.ds(GOT, 2 * NODE)], proj[pl.ds(GOT, 2 * NODE), :]
     )
 
+    loads["wn_in"].wait()
+    total[...] = dot(x, wn_in[pl.ds(0, D), :])
     for one in nears:
         one.wait_recv()
     far_all.wait_recv()
     xe[pl.ds(0, NEAR), :] = near_got[...].reshape(NEAR, D)
     slot = lax.broadcasted_iota(jnp.int32, (FAR, 4, 128), 0)
-    far_rows = jnp.where(slot == me, far_src[...], far_got[...]).reshape(FAR, D)
+    far_rows = jnp.where(slot == me, far_src[...].reshape(FAR, 4, 128), far_got[...]).reshape(FAR, D)
     xe[pl.ds(NEAR, FAR), :] = far_rows
     xe[pl.ds(NEAR + FAR, 96), :] = jnp.zeros((96, D), BF)
     proj[pl.ds(0, GOT), :] = dot(xe[pl.ds(0, GOT), :], we_in[pl.ds(0, D), :]).astype(BF)
 
     loads["we_out"].wait()
 
-    for k in range(EDGE // TILE):
-        at = pl.ds(k * TILE, TILE)
-        v = pre[at, :] + dot(onehot[at, pl.ds(0, GOT)], proj[pl.ds(0, GOT), :])
+    count = EDGE // TILE
+    tiles = [pl.ds(k * TILE, TILE) for k in range(count)]
+
+    def enter(k):
+        return pre[tiles[k], :] + dot(onehot[tiles[k], pl.ds(0, GOT)], proj[pl.ds(0, GOT), :])
+
+    def activate(k, v):
         s = jax.nn.sigmoid(v)
         h = (v * s).astype(BF)
-        hid[at, :] = h
-        pre[at, :] = s * (1.0 + v * (1.0 - s))
-        normed, inverse = normalize(dot(h, we_out[...]))
-        msg[at, :] = normed.astype(BF)
-        inv[at, :] = jnp.broadcast_to(inverse, (TILE, 128))
+        hid[tiles[k], :] = h
+        pre[tiles[k], :] = s * (1.0 + v * (1.0 - s))
+        return dot(h, we_out[...])
+
+    def settle(k, out):
+        normed, inverse = normalize(out)
+        msg[tiles[k], :] = normed.astype(BF)
+        inv[tiles[k], :] = jnp.broadcast_to(inverse, (TILE, 128))
+
+    v, out = enter(0), None
+    for k in range(count):
+        v_next = enter(k + 1) if k + 1 < count else None
+        out_next = activate(k, v)
+        if out is not None:
+            settle(k - 1, out)
+        v, out = v_next, out_next
+    settle(count - 1, out)
 
     aggregate = dot(onehot_t[pl.ds(EXT, NODE), :], msg[...]).astype(BF)
 
-    loads["wn_in"].wait()
-    node_pre = dot(x, wn_in[pl.ds(0, D), :]) + dot(aggregate, wn_in[pl.ds(D, D), :])
+    node_pre = total[...] + dot(aggregate, wn_in[pl.ds(D, D), :])
     s = jax.nn.sigmoid(node_pre)
     node_hidden = (node_pre * s).astype(BF)
     node_slope = s * (1.0 + node_pre * (1.0 - s))
@@ -354,7 +377,9 @@
     node_z_grad = norm_back(updated_grad, node_normed, node_inverse).astype(BF)
     node_pre_grad = (dot_t(node_z_grad, wn_out[...]) * node_slope).astype(BF)
     total[...] = updated_grad + dot_t(node_pre_grad, wn_in[pl.ds(0, D), :])
-    agg_grad[...] = dot_t(node_pre_grad, wn_in[pl.ds(D, D), :]).astype(BF)
+    aggregate_grad = dot_t(node_pre_grad, wn_in[pl.ds(D, D), :])
+    centre = jnp.mean(aggregate_grad, axis=-1, keepdims=True)
+    agg_grad[...] = (aggregate_grad - centre).astype(BF)
 
     where = (ix, iy, iz, ic)
     ga, gb = Reducer(group_a, where), Reducer(group_b, where)
@@ -380,25 +405,38 @@
             ga.start0[1, c, y, :, :, 1] = readout[:, :, c].astype(BF)
     ga.pair()
 
-    def edge_backward(k):
-        at = pl.ds(k * TILE, TILE)
-        g = dot(onehot[at, pl.ds(EXT, NODE)], agg_grad[...])
-        z_grad = norm_back(g, msg[at, :].astype(F32), inv[at, :][:, 0:1]).astype(BF)
-        ezg[at, :] = z_grad
-        epg[at, :] = (dot_t(z_grad, we_out[...]) * pre[at, :]).astype(BF)
-
-    for k in range(EDGE // TILE):
-        edge_backward(k)
+    def gather(k):
+        return dot(onehot[tiles[k], pl.ds(EXT, NODE)], agg_grad[...])
+
+    def norm_step(k, g):
+        y = msg[tiles[k], :].astype(F32)
+        second = jnp.mean(g * y, axis=-1, keepdims=True)
+        z_grad = (inv[tiles[k], :][:, 0:1] * (g - y * second)).astype(BF)
+        ezg[tiles[k], :] = z_grad
+        return dot_t(z_grad, we_out[...])
+
+    def slope_step(k, out):
+        epg[tiles[k], :] = (out * pre[tiles[k], :]).astype(BF)
+
+    g, out = gather(0), None
+    for k in range(count):
+        g_next = gather(k + 1) if k + 1 < count else None
+        out_next = norm_step(k, g)
+        if out is not None:
+            slope_step(k - 1, out)
+        g, out = g_next, out_next
         if k == 2:
             ga.first()
+    slope_step(count - 1, out)
+
     gsum[...] = dot(onehot_t[...], epg[...]).astype(BF)
+
+    wgrad[pl.ds(2 * D, D), :] = t_dot(e[...], epg[...])
+    pack_rows(gb.start0, t_dot(hid[...], ezg[...]), 1, ((1, 1),))
     ga.middle()
-
     wgrad[pl.ds(0, D), :] = t_dot(xe[...], gsum[pl.ds(0, EXT), :])
     wgrad[pl.ds(D, D), :] = t_dot(x, gsum[pl.ds(EXT, NODE), :])
-    wgrad[pl.ds(2 * D, D), :] = t_dot(e[...], epg[...])
     pack_rows(gb.start0, wgrad[...], 3, ((0, 0), (0, 1), (1, 0)))
-    pack_rows(gb.start0, t_dot(hid[...], ezg[...]), 1, ((1, 1),))
     gb.pair()
     back = dot_t(gsum[pl.ds(0, GOT), :], we_in[pl.ds(0, D), :])
     back_near_src[...] = back[0:NEAR].astype(BF).reshape(6, 16, D)
@@ -432,9 +470,7 @@
         ))
     back_far_mid[pl.ds(iz, 1)] = back_far_src[:, pl.ds(iz, 1)].reshape(1, 4, 2, 4, 128)
 
-    edge_res[...] = dot_t(epg[...], we_in[pl.ds(2 * D, D), :]).astype(BF)
-    edge_copy = pltpu.make_async_copy(edge_res, edge_out.at[0], out_sem.at[0])
-    edge_copy.start()
+    edge_out[0] = dot_t(epg[...], we_in[pl.ds(2 * D, D), :]).astype(BF)
     gb.first()
     ga.second()
     total[...] += dot_t(gsum[pl.ds(GOT, NODE), :], we_in[pl.ds(0, D), :]) + dot_t(
@@ -460,9 +496,7 @@
         one.wait_recv()
     far_rows = back_far_got[...].reshape(FAR, D)
     owned = dot(own_near[...], back_near_got[...].reshape(NEAR, D)) + dot(own_far[...], far_rows)
-    node_res[...] = (total[...] + owned).astype(BF)
-    node_copy = pltpu.make_async_copy(node_res, node_out.at[0], out_sem.at[1])
-    node_copy.start()
+    node_out[0] = (total[...] + owned).astype(BF)
 
     gb.third()
     ga.fourth()
@@ -470,24 +504,19 @@
     parts = ga.last()
     for y in range(4):
         at = pl.ds(y * 128, 128)
-        grads[pl.ds(32, 8), at] = parts[y][0, 0]
-        grads[pl.ds(40, 8), at] = parts[y][0, 1]
-        grads[pl.ds(48, 8), at] = parts[y][1, 0]
-    grads[pl.ds(56, 8), pl.ds(0, 128)] = parts[0][1, 1]
-    grads[pl.ds(56, 8), pl.ds(128, 384)] = jnp.zeros((8, 384), F32)
+        grads_out[pl.ds(32, 8), at] = parts[y][0, 0]
+        grads_out[pl.ds(40, 8), at] = parts[y][0, 1]
+        grads_out[pl.ds(48, 8), at] = parts[y][1, 0]
+    grads_out[pl.ds(56, 8), pl.ds(0, 128)] = parts[0][1, 1]
+    grads_out[pl.ds(56, 8), pl.ds(128, 384)] = jnp.zeros((8, 384), F32)
     parts = gb.last()
     for y in range(4):
         at = pl.ds(y * 128, 128)
-        grads[pl.ds(0, 8), at] = parts[y][0, 0]
-        grads[pl.ds(8, 8), at] = parts[y][0, 1]
-        grads[pl.ds(16, 8), at] = parts[y][1, 0]
-        grads[pl.ds(24, 8), at] = parts[y][1, 1]
-    grads_copy = pltpu.make_async_copy(grads, grads_out, dma_sem.at[0])
-    grads_copy.start()
-
-    grads_copy.wait()
-    node_copy.wait()
-    edge_copy.wait()
+        grads_out[pl.ds(0, 8), at] = parts[y][0, 0]
+        grads_out[pl.ds(8, 8), at] = parts[y][0, 1]
+        grads_out[pl.ds(16, 8), at] = parts[y][1, 0]
+        grads_out[pl.ds(24, 8), at] = parts[y][1, 1]
+
     for one in nears + backs + bfars:
         one.wait_send()
     far_all.wait_send()
@@ -496,24 +525,14 @@
 
 
 def hand_out(node, edge, grads, *rest):
-    outs, (node_v, edge_v, grads_v, take_sem, give_sem) = rest[:7], rest[7:]
+    outs, sems = rest[:7], rest[7]
     parts = ((0, 24, D), (24, 8, D), (32, 16, D), (48, 8, D), (56, 8, 128))
-    steps = [(grads, grads_v, [
-        (grads_v.at[pl.ds(at, n), pl.ds(0, w)], outs[2 + k]) for k, (at, n, w) in enumerate(parts)
-    ])]
-    for k in range(5):
-        at = pl.ds(k * TILE, TILE)
-        steps.append((edge.at[0, at], edge_v.at[at], [(edge_v.at[at], outs[1].at[0, at])]))
-    steps.append((node.at[0], node_v, [(node_v, outs[0].at[0])]))
-    takes, gives = [], []
-    for k, (src, dst, _) in enumerate(steps):
-        takes.append(pltpu.make_async_copy(src, dst, take_sem.at[k]))
-        takes[-1].start()
-    for k, (_, _, moves) in enumerate(steps):
-        takes[k].wait()
-        for src, dst in moves:
-            gives.append(pltpu.make_async_copy(src, dst, give_sem.at[len(gives)]))
-            gives[-1].start()
+    moves = [(edge, outs[1]), (node, outs[0])] + [
+        (grads.at[pl.ds(at, n), pl.ds(0, w)], outs[2 + k]) for k, (at, n, w) in enumerate(parts)
+    ]
+    gives = [pltpu.make_async_copy(src, dst, sems.at[k]) for k, (src, dst) in enumerate(moves)]
+    for one in gives:
+        one.start()
     for one in gives:
         one.wait()
 
@@ -541,8 +560,8 @@
 
 def body(*args):
     (x, e, t, we_in, we_out, wn_in, wn_out, wr, send, far, sender, receiver, count, land, lat) = args
-    anywhere = pl.BlockSpec(memory_space=pl.ANY)
     hbm = pl.BlockSpec(memory_space=pltpu.HBM)
+    vmem = pl.BlockSpec(memory_space=pltpu.VMEM)
     near = pltpu.VMEM((6, 16, D), BF)
     row = pltpu.VMEM((FAR, 4, 128), BF)
     natural = pltpu.VMEM((4, 8, 2, 4, 128), BF)
@@ -563,8 +582,7 @@
         pltpu.VMEM((2 * D, D), BF),
         pltpu.VMEM((D, D), BF),
         pltpu.VMEM((D, 128), BF),
-        pltpu.VMEM((EDGE, D), BF),
-        near, near, row, row, near, near, natural, turned, natural,
+        near, near, natural, row, near, near, natural, turned, natural,
         pltpu.VMEM((EDGE, TABLE), BF),
         pltpu.VMEM((TABLE, EDGE), BF),
         pltpu.VMEM((NODE, NEAR), BF),
@@ -580,9 +598,7 @@
         pltpu.VMEM((NODE, D), BF),
         pltpu.VMEM((TABLE, D), BF),
         pltpu.VMEM((3 * D, D), F32),
-        pltpu.VMEM((NODE, D), BF),
-        pltpu.VMEM((64, D), F32),
-        sem((14,)), sem((2,)),
+        sem((14,)),
         sem((6,)), sem((6,)), sem((1,)), sem((1,)),
         sem((6,)), sem((6,)), sem((14,)), sem((14,)),
     ] + group_scratch() + group_scratch()
@@ -597,30 +613,24 @@
     )
     results = pl.pallas_call(
         kernel,
-        out_shape=(*shapes[:2], jax.ShapeDtypeStruct((64, D), F32)),
+        out_shape=(pltpu.VMEM((1, NODE, D), BF), pltpu.VMEM((1, EDGE, D), BF), pltpu.VMEM((64, D), F32)),
         in_specs=[hbm] * 12 + [pl.BlockSpec(memory_space=pltpu.SMEM)] + [hbm] * 2,
-        out_specs=(anywhere,) * 3,
+        out_specs=(vmem,) * 3,
         scratch_shapes=scratch,
         compiler_params=pltpu.CompilerParams(
-            collective_id=0, has_side_effects=True, vmem_limit_bytes=62 * 1024 * 1024
+            collective_id=0, has_side_effects=True, vmem_limit_bytes=50 * 1024 * 1024
         ),
-    )(
-        x, e, t, we_in, we_out, wn_in, wn_out, wr, send, far,
-        sender, receiver, count, land, lat,
-    )
+    )(*(
+        a if a is count else pltpu.with_memory_space_constraint(a, pltpu.HBM)
+        for a in args
+    ))
     return pl.pallas_call(
         hand_out,
         out_shape=shapes,
-        in_specs=[anywhere] * 3,
+        in_specs=[vmem] * 3,
         out_specs=(hbm,) * 7,
-        scratch_shapes=[
-            pltpu.VMEM((NODE, D), BF),
-            pltpu.VMEM((EDGE, D), BF),
-            pltpu.VMEM((64, D), F32),
-            sem((7,)),
-            sem((11,)),
-        ],
-        compiler_params=pltpu.CompilerParams(vmem_limit_bytes=60 * 1024 * 1024),
+        scratch_shapes=[sem((7,))],
+        compiler_params=pltpu.CompilerParams(vmem_limit_bytes=3072 * 1024),
     )(*results)
 
 

time: 65.6 us -> 59.9 us (0.913)
  Pallas kernels: 64 us -> 58.4 us
    pallas_call x2, Pallas kernels: 64 us -> 58.4 us  [the longest x1 57.1 us: body(): pl.pallas_call(kernel, out_shape=(pltpu.VMEM((1, NODE, D), BF), pltpu.VME...]
where the time goes in v2:
time: 59.9 us; the launch traced here: 59.8 us
  Pallas kernels  58.4 us (97%)
  between operations  1.45 us (2%)
    pallas_call x1, Pallas kernels, body(): pl.pallas_call(kernel, out_shape=(pltpu.VMEM((1, NODE, D), BF), pltpu.VME...  57.1 us
    pallas_call x1, Pallas kernels, body(): pl.pallas_call(hand_out, out_shape=shapes, in_specs=[vmem] * 3, out_specs...  1.27 us

profile of v2, /device:TPU:8, one launch (start us, length us, event | category | flops | bytes accessed | tf_op | source)
XLA Modules:
  0.0 59.8 jit_solution(11736821857212139502)
XLA Ops:
  1.3 57.1 %shard_map.198 = (bf16[1,384,512]{2,1,0:T(8,128)(2,1)S(1)}, bf16[1,1280,512]{2,1,0:T(8,128)(2,1)S(1)}, f32[64,512]{1,0:T(8,128)S(1)}) custom-call(bf16[1,384,512]{2,1,0:T(8,128)(2,1)} %x_hbm.1, bf16[1,1280,512]{2,1,0:T(8,128)(2,1)} %e_hbm.1, bf16[1,384,128]{2,1,0:T(8,128)(2,1)} %t_hbm.1, bf16[1536,512]{1,0:T(8,128)(2,1)} %we_in_hbm.1, ...), custom_call_target="tpu_custom_call" | custom-call | tf_op jit(solution)/shard_map/pallas_call | solution.py:614
  58.4 1.3 %shard_map.199 = (bf16[1,384,512]{2,1,0:T(8,128)(2,1)}, bf16[1,1280,512]{2,1,0:T(8,128)(2,1)}, f32[24,512]{1,0:T(8,128)}, f32[8,512]{1,0:T(8,128)}, f32[16,512]{...) custom-call(bf16[1,384,512]{2,1,0:T(8,128)(2,1)S(1)} %get-tuple-element.10.node, ...), custom_call_target="tpu_custom_call" | custom-call | tf_op jit(solution)/shard_map/pallas_call | solution.py:627

commit v3 on v2

--- a/solution.py
+++ b/solution.py
@@ -21,6 +21,7 @@
 GOT = EXT - NODE
 TABLE = EXT + NODE
 TILE = 256
+ROWS = 1
 OFFSETS = (1, -1, 2, -2, 3, -3)
 BF = jnp.bfloat16
 F32 = jnp.float32
@@ -103,35 +104,44 @@
             axis, at = self.axes[h][0]
             right, left, across = (at + 1) % 4, (at + 3) % 4, (at + 2) % 4
             lo, hi = pl.ds(0, 2), pl.ds(2, 2)
-            w1, k = self.w1, 2 + 6 * h
-            self.c1.append((
-                self.copy(w1.at[h, across, lo], self.relay.at[h, 0], k, {axis: right}),
-                self.copy(w1.at[h, across, hi], self.relay.at[h, 1], k + 1, {axis: left}),
-                self.copy(w1.at[h, left, lo], self.direct.at[h, 0], k + 2, {axis: left}),
-                self.copy(w1.at[h, right, hi], self.direct.at[h, 1], k + 3, {axis: right}),
-            ))
+            w1, k = self.w1, 2 + 10 * h
+            ends = (right, left)
+            relays = [
+                self.copy(
+                    w1.at[h, across, 2 * side + j], self.relay.at[h, side, j], k + 2 * j + side,
+                    {axis: ends[side]},
+                )
+                for j in range(2)
+                for side in range(2)
+            ]
+            self.c1.append((relays, (
+                self.copy(w1.at[h, left, lo], self.direct.at[h, 0], k + 4, {axis: left}),
+                self.copy(w1.at[h, right, hi], self.direct.at[h, 1], k + 5, {axis: right}),
+            )))
 
     def middle(self):
         self.c1b = []
-        for h in range(2):
-            axis, at = self.axes[h][0]
-            ends = ((at + 1) % 4, (at + 3) % 4)
-            for side in range(2):
-                self.c1[h][side].wait_recv()
-                mine = self.w1[h, ends[side], pl.ds(2 * side, 2)].astype(F32)
-                self.merged[h, side] = (mine + self.relay[h, side].astype(F32)).astype(BF)
-                self.c1b.append(self.copy(
-                    self.merged.at[h, side], self.carried.at[h, side], 6 + 6 * h + side,
-                    {axis: ends[side]},
-                ))
+        for j in range(2):
+            for h in range(2):
+                axis, at = self.axes[h][0]
+                ends = ((at + 1) % 4, (at + 3) % 4)
+                for side in range(2):
+                    self.c1[h][0][2 * j + side].wait_recv()
+                    mine = self.w1[h, ends[side], 2 * side + j].astype(F32)
+                    self.merged[h, side, j] = (mine + self.relay[h, side, j].astype(F32)).astype(BF)
+                    self.c1b.append(self.copy(
+                        self.merged.at[h, side, j], self.carried.at[h, side, j],
+                        8 + 10 * h + 2 * j + side, {axis: ends[side]},
+                    ))
 
     def second(self):
         self.c2 = []
         for h in range(2):
             _, own = self.axes[h][0]
             for side in range(2):
-                self.c1[h][2 + side].wait_recv()
-                self.c1b[2 * h + side].wait_recv()
+                self.c1[h][1][side].wait_recv()
+                for j in range(2):
+                    self.c1b[4 * j + 2 * h + side].wait_recv()
                 part = pl.ds(2 * side, 2)
                 acc = self.w1[h, own, part].astype(F32) + self.direct[h, side].astype(F32)
                 self.w2[h, part] = (acc + self.carried[h, side].astype(F32)).astype(BF)
@@ -139,7 +149,7 @@
             for d in range(1, 4):
                 to = (at + d) % 4
                 self.c2.append(
-                    self.copy(self.w2.at[h, to], self.r2.at[h, d - 1], 13 + 3 * h + d, {axis: to})
+                    self.copy(self.w2.at[h, to], self.r2.at[h, d - 1], 21 + 3 * h + d, {axis: to})
                 )
 
     def third(self):
@@ -153,7 +163,7 @@
         self.c3 = []
         for d in range(1, 8):
             to = (self.z + d) % 8
-            self.c3.append(self.copy(self.w3.at[to], self.r3.at[d - 1], 19 + d, {"patch_1": to}))
+            self.c3.append(self.copy(self.w3.at[to], self.r3.at[d - 1], 27 + d, {"patch_1": to}))
 
     def fourth(self):
         for one in self.c3:
@@ -165,7 +175,7 @@
         self.c4 = []
         for d in range(1, 4):
             to = (self.y + d) % 4
-            self.c4.append(self.copy(self.w4, self.r4.at[d - 1], 26 + d, {"rep": to}))
+            self.c4.append(self.copy(self.w4, self.r4.at[d - 1], 34 + d, {"rep": to}))
 
     def last(self):
         for one in self.c4:
@@ -193,6 +203,7 @@
     xe, e, tgt, we_in, we_out, wn_in, wn_out, wr,
     near_src, near_got, far_src, far_got, back_near_src, back_near_got, back_far_src, back_far_mid, back_far_got,
     onehot, onehot_t, own_near, own_far, proj, pre, hid, msg, inv, ezg, epg, total, agg_grad, gsum, wgrad,
+    aggr, node_hid, fresh, nzg, npg, miss, weights,
     *rest,
 ):
     dma_sem, near_send, near_recv, far_send, far_recv = rest[:5]
@@ -219,7 +230,8 @@
         ("lat", lat_hbm, lat_ref),
     )):
         loads[name] = pltpu.make_async_copy(src, dst, dma_sem.at[k])
-        loads[name].start()
+        if k in (0, 1, 4):
+            loads[name].start()
 
     barrier = pltpu.get_barrier_semaphore()
 
@@ -236,6 +248,10 @@
 
     for d in range(1, 4):
         greet(barrier, {"rep": (iy + d) % 4})
+
+    for name in loads:
+        if name not in ("send", "far", "x"):
+            loads[name].start()
 
     loads["send"].wait()
     loads["far"].wait()
@@ -312,6 +328,12 @@
         onehot[:, pl.ds(GOT, 2 * NODE)], proj[pl.ds(GOT, 2 * NODE), :]
     )
 
+    loads["land"].wait()
+    loads["lat"].wait()
+    latitude = -0.5 * jnp.pi + (lat_ref[...].reshape(1, NODE).astype(F32) + 0.5) * (jnp.pi / BANDS)
+    cols = columns([jnp.cos(latitude), land_ref[...].reshape(1, NODE).astype(F32)])
+    channel = lax.broadcasted_iota(jnp.int32, (NODE, 128), 1)
+    weights[...] = jnp.where((channel < OCEAN) & (cols[:, 1:2] == 1.0), 0.0, cols[:, 0:1])
     loads["wn_in"].wait()
     total[...] = dot(x, wn_in[pl.ds(0, D), :])
     for one in nears:
@@ -355,31 +377,44 @@
 
     aggregate = dot(onehot_t[pl.ds(EXT, NODE), :], msg[...]).astype(BF)
 
-    node_pre = total[...] + dot(aggregate, wn_in[pl.ds(D, D), :])
-    s = jax.nn.sigmoid(node_pre)
-    node_hidden = (node_pre * s).astype(BF)
-    node_slope = s * (1.0 + node_pre * (1.0 - s))
+    aggr[...] = aggregate
+    span = NODE // ROWS
+    parts = [pl.ds(k * span, span) for k in range(ROWS)]
     loads["wn_out"].wait()
-    node_normed, node_inverse = normalize(dot(node_hidden, wn_out[...]))
-    updated = (x.astype(F32) + node_normed).astype(BF)
     loads["wr"].wait()
-    predicted = dot(updated, wr[...])
-    loads["land"].wait()
-    loads["lat"].wait()
-    latitude = -0.5 * jnp.pi + (lat_ref[...].reshape(1, NODE).astype(F32) + 0.5) * (jnp.pi / BANDS)
-    cols = columns([jnp.cos(latitude), land_ref[...].reshape(1, NODE).astype(F32)])
-    area, land = cols[:, 0:1], cols[:, 1:2]
-    channel = lax.broadcasted_iota(jnp.int32, (NODE, 128), 1)
-    weight = jnp.where((channel < OCEAN) & (land == 1.0), 0.0, area)
     loads["t"].wait()
-    pred_grad = (weight * (predicted - tgt[...].astype(F32))).astype(BF)
-    updated_grad = dot_t(pred_grad, wr[...])
-    node_z_grad = norm_back(updated_grad, node_normed, node_inverse).astype(BF)
-    node_pre_grad = (dot_t(node_z_grad, wn_out[...]) * node_slope).astype(BF)
-    total[...] = updated_grad + dot_t(node_pre_grad, wn_in[pl.ds(0, D), :])
-    aggregate_grad = dot_t(node_pre_grad, wn_in[pl.ds(D, D), :])
-    centre = jnp.mean(aggregate_grad, axis=-1, keepdims=True)
-    agg_grad[...] = (aggregate_grad - centre).astype(BF)
+    def bend(p):
+        node_pre = total[p, :] + dot(aggr[p, :], wn_in[pl.ds(D, D), :])
+        s = jax.nn.sigmoid(node_pre)
+        node_hid[p, :] = (node_pre * s).astype(BF)
+        return s * (1.0 + node_pre * (1.0 - s))
+
+    def lift(p):
+        normed, inverse = normalize(dot(node_hid[p, :], wn_out[...]))
+        fresh[p, :] = (xe[pl.ds(GOT + p.start, span), :].astype(F32) + normed).astype(BF)
+        return normed, inverse
+
+    def judge(p):
+        weight = weights[p, :]
+        grad = weight * (dot(fresh[p, :], wr[...]) - tgt[p, :].astype(F32))
+        miss[p, :] = grad.astype(BF)
+        return dot_t(miss[p, :], wr[...])
+
+    def lower(p, grad, normed, inverse):
+        nzg[p, :] = norm_back(grad, normed, inverse).astype(BF)
+        return dot_t(nzg[p, :], wn_out[...])
+
+    slopes = [bend(p) for p in parts]
+    norms = [lift(p) for p in parts]
+    grads = [judge(p) for p in parts]
+    downs = [lower(p, g, *n) for p, g, n in zip(parts, grads, norms)]
+    for p, down, slope in zip(parts, downs, slopes):
+        npg[p, :] = (down * slope).astype(BF)
+    for p, grad in zip(parts, grads):
+        aggregate_grad = dot_t(npg[p, :], wn_in[pl.ds(D, D), :])
+        centre = jnp.mean(aggregate_grad, axis=-1, keepdims=True)
+        agg_grad[p, :] = (aggregate_grad - centre).astype(BF)
+        total[p, :] = grad + dot_t(npg[p, :], wn_in[pl.ds(0, D), :])
 
     where = (ix, iy, iz, ic)
     ga, gb = Reducer(group_a, where), Reducer(group_b, where)
@@ -395,11 +430,11 @@
                     else:
                         start0[h, c, y, :, :, t] = tile
 
-    wgrad[pl.ds(0, D), :] = t_dot(x, node_pre_grad)
-    wgrad[pl.ds(D, D), :] = t_dot(aggregate, node_pre_grad)
+    wgrad[pl.ds(0, D), :] = t_dot(x, npg[...])
+    wgrad[pl.ds(D, D), :] = t_dot(aggr[...], npg[...])
     pack_rows(ga.start0, wgrad[pl.ds(0, 2 * D), :], 2, ((0, 0), (0, 1)))
-    pack_rows(ga.start0, t_dot(node_hidden, node_z_grad), 1, ((1, 0),))
-    readout = t_dot(updated, pred_grad).reshape(4, 8, 2, 8, 128)
+    pack_rows(ga.start0, t_dot(node_hid[...], nzg[...]), 1, ((1, 0),))
+    readout = t_dot(fresh[...], miss[...]).reshape(4, 8, 2, 8, 128)
     for c in range(2):
         for y in range(4):
             ga.start0[1, c, y, :, :, 1] = readout[:, :, c].astype(BF)
@@ -425,7 +460,7 @@
         if out is not None:
             slope_step(k - 1, out)
         g, out = g_next, out_next
-        if k == 2:
+        if k == (count + 1) // 2 - 1:
             ga.first()
     slope_step(count - 1, out)
 
@@ -553,8 +588,8 @@
         pltpu.VMEM((7, 2, 2, *tail), BF),
         pltpu.VMEM((2, 2, *tail), F32),
         pltpu.VMEM((3, 2, 2, *tail), F32),
-        pltpu.SemaphoreType.DMA((30,)),
-        pltpu.SemaphoreType.DMA((30,)),
+        pltpu.SemaphoreType.DMA((38,)),
+        pltpu.SemaphoreType.DMA((38,)),
     ]
 
 
@@ -563,6 +598,7 @@
     hbm = pl.BlockSpec(memory_space=pltpu.HBM)
     vmem = pl.BlockSpec(memory_space=pltpu.VMEM)
     near = pltpu.VMEM((6, 16, D), BF)
+    node = pltpu.VMEM((NODE, D), BF)
     row = pltpu.VMEM((FAR, 4, 128), BF)
     natural = pltpu.VMEM((4, 8, 2, 4, 128), BF)
     turned = pltpu.VMEM((8, 4, 2, 4, 128), BF)
@@ -598,6 +634,7 @@
         pltpu.VMEM((NODE, D), BF),
         pltpu.VMEM((TABLE, D), BF),
         pltpu.VMEM((3 * D, D), F32),
+        node, node, node, node, node, pltpu.VMEM((NODE, 128), BF), pltpu.VMEM((NODE, 128), F32),
         sem((14,)),
         sem((6,)), sem((6,)), sem((1,)), sem((1,)),
         sem((6,)), sem((6,)), sem((14,)), sem((14,)),

time: 59.9 us -> 59.6 us (level)
  no operation moved by 1% of the time
where the time goes in v3:
time: 59.6 us; the launch traced here: 59.5 us
  Pallas kernels  58.1 us (97%)
  between operations  1.45 us (2%)
    pallas_call x1, Pallas kernels, body(): pl.pallas_call(kernel, out_shape=(pltpu.VMEM((1, NODE, D), BF), pltpu.VME...  56.8 us
    pallas_call x1, Pallas kernels, body(): pl.pallas_call(hand_out, out_shape=shapes, in_specs=[vmem] * 3, out_specs...  1.27 us

profile of v3, /device:TPU:8, one launch (start us, length us, event | category | flops | bytes accessed | tf_op | source)
XLA Modules:
  0.0 59.5 jit_solution(11109699905262628746)
XLA Ops:
  1.3 56.8 %shard_map.198 = (bf16[1,384,512]{2,1,0:T(8,128)(2,1)S(1)}, bf16[1,1280,512]{2,1,0:T(8,128)(2,1)S(1)}, f32[64,512]{1,0:T(8,128)S(1)}) custom-call(bf16[1,384,512]{2,1,0:T(8,128)(2,1)} %x_hbm.1, bf16[1,1280,512]{2,1,0:T(8,128)(2,1)} %e_hbm.1, bf16[1,384,128]{2,1,0:T(8,128)(2,1)} %t_hbm.1, bf16[1536,512]{1,0:T(8,128)(2,1)} %we_in_hbm.1, ...), custom_call_target="tpu_custom_call" | custom-call | tf_op jit(solution)/shard_map/pallas_call | solution.py:651
  58.1 1.3 %shard_map.199 = (bf16[1,384,512]{2,1,0:T(8,128)(2,1)}, bf16[1,1280,512]{2,1,0:T(8,128)(2,1)}, f32[24,512]{1,0:T(8,128)}, f32[8,512]{1,0:T(8,128)}, f32[16,512]{...) custom-call(bf16[1,384,512]{2,1,0:T(8,128)(2,1)S(1)} %get-tuple-element.10.node, ...), custom_call_target="tpu_custom_call" | custom-call | tf_op jit(solution)/shard_map/pallas_call | solution.py:664
